TPU v7x, 32 devices: a whole 2x2x4 slice. The times are simulated.
32 devices in a mesh: occ: 4 (over x, core), vir: 8 (over z, y).
Axes of the slice: x: 2, y: 2, z: 4, core: 2. Of those that a mesh axis runs over, the one named last changes fastest.
Arguments:
- factor: float32 [4, 4096, 1280], P('occ', 'vir'), may hold values from -0.6 to 0.6
- occ_energy: float32 [4], P('occ'), may hold values from -2 to -0.5
- vir_energy: float32 [4096], P('vir'), may hold values from 0.2 to 4.7
Outputs:
- aux_density: float32 [4, 4096, 1280], P('occ', 'vir')
- pair_trace: float32 [4, 3], P('occ')
All inputs are finite; a program needn't handle non-finite values.
Results may differ from a plain program's by a relative error of at most 0.00013.
Values sent between devices are 32-bit elements; how exact they have to be, the bound alone decides.
No kernel may reach another device: no remote copies, remote signals or barrier semaphores. Data moves between devices by JAX's collectives and lax.ppermute only.
A program may use at most 128 MiB of HBM per device.

v0:
```python
import functools

import jax
import jax.numpy as jnp
from jax import lax
from jax.experimental import pallas as pl
from jax.experimental.pallas import tpu as pltpu
from jax.sharding import PartitionSpec as P


STEPS = 3
AXES = ("occ", "vir")
F32, BF16 = jnp.float32, jnp.bfloat16
VMEM_LIMIT = 12 * 2**20


def permuted(value, move):
    occs, virs = lax.axis_size("occ"), lax.axis_size("vir")
    route = []
    for i in range(occs):
        for v in range(virs):
            source = move(i, v)
            route.append((source[0] % occs * virs + source[1], i * virs + v))
    return lax.ppermute(value, AXES, route)


def weight(offset, occs):
    return sum(offset == k % occs for k in range(STEPS)) + sum(
        offset == -k % occs for k in range(STEPS)
    )


def split(value):
    high = value.astype(BF16)
    return high, (value - high.astype(F32)).astype(BF16)


def dot(former, latter, transposed):
    contracted = ((1,), (1 if transposed else 0,))
    return lax.dot_general(
        former, latter, (contracted, ((), ())), preferred_element_type=F32
    )


def product(former, latter, transposed):
    (fh, fl), (lh, ll) = former, latter
    return dot(fh, lh, transposed) + dot(fh, ll, transposed) + dot(fl, lh, transposed)


def column(row):
    return jnp.transpose(jnp.broadcast_to(row, (8, row.shape[1])))[:, :1]


def lanes(value):
    return jnp.sum(value, axis=0, keepdims=True)


def is_odd():
    return lax.rem(lax.axis_index("occ"), 2)


def each(rows, body, count=2):
    size = rows // count

    def step(m, carry):
        body(pl.ds(pl.multiple_of(m * size, size), size))
        return carry

    lax.fori_loop(0, count, step, 0)


def put_split(high, low, rows):
    def step(m):
        high[m], low[m] = split(rows[m])

    each(rows.shape[0], step, 4)


def start_kernel(weights, e0, e1, vir, own, near, total, blocks_h, blocks_l, traces,
                 col, amp, bar_h, bar_l):
    n = own.shape[0]
    put_split(blocks_h.at[0], blocks_l.at[0], own)
    put_split(blocks_h.at[1], blocks_l.at[1], near)
    total[...] = jnp.zeros(total.shape, F32)
    traces[...] = jnp.zeros(traces.shape, F32)

    def block(k, carry):
        pair = e0[0] + jnp.where(k == 0, e0[0], e1[0])
        scale = jnp.where(k == 0, float(weights[0]), float(weights[1]))
        col[...] = pair - column(vir[...])

        def amps(m):
            amp[m] = product((blocks_h[0, m], blocks_l[0, m]), (blocks_h[k], blocks_l[k]), True) / (
                col[m] - vir[...])

        each(n, amps)
        bar = 2.0 * amp[...] - amp[...].T
        traces[pl.ds(k, 1)] = lanes(amp[...] * bar)
        bar_h[...], bar_l[...] = split(scale * bar)

        def totals(m):
            total[m] += product((bar_h[m], bar_l[m]), (blocks_h[k], blocks_l[k]), False)

        each(n, totals)
        return carry

    lax.fori_loop(0, 2, block, 0)


def first_kernel(weights, e0, e1, e2, e3, vir, far, blocks_h, blocks_l, first, first_core, before,
                 traces_in, total, firsts_h, firsts_l, far_amp, traces, col, amp, bar_h, bar_l):
    n = first.shape[0]
    odd = is_odd()
    put_split(firsts_h.at[0], firsts_l.at[0], first)
    put_split(firsts_h.at[1], firsts_l.at[1], first_core)
    pair = e0[0] + jnp.where(odd == 0, e2[0], e3[0])
    pair_far = e0[0] + jnp.where(odd == 0, e1[0], e0[0])
    scale = jnp.where(odd == 0, float(weights[2]), float(weights[1]))
    col[...] = column(vir[...])

    def amps(m):
        left = (blocks_h[0, m], blocks_l[0, m])
        amp[m] = product(left, (firsts_h[odd], firsts_l[odd]), True) / (pair - col[m] - vir[...])
        far_amp[m] = product(left, (firsts_h[1 - odd], firsts_l[1 - odd]), True) / (
            pair_far - col[m] - far[...])

    each(n, amps)
    bar = 2.0 * amp[...] - amp[...].T
    traces[...] = traces_in[...]
    traces[pl.ds(2 + odd, 1)] = lanes(amp[...] * bar)
    bar_h[...], bar_l[...] = split(scale * bar)

    def totals(m):
        total[m] = before[m] + product((bar_h[m], bar_l[m]), (firsts_h[odd], firsts_l[odd]), False)

    each(n, totals)


def middle_kernel(e0, e2, vir, far, blocks_h, blocks_l, firsts_h, firsts_l, far_amp, second,
                  pair_h, pair_l, amps, col):
    n = second.shape[0]
    odd = is_odd()
    put_split(pair_h.at[odd], pair_l.at[odd], second)
    pair_h[1 - odd], pair_l[1 - odd] = firsts_h[1 - odd], firsts_l[1 - odd]
    amps[1 - odd] = far_amp[...]
    col[...] = column(vir[...])
    row = jnp.where(odd == 0, far[...], vir[...])
    pair = e0[0] + jnp.where(odd == 0, e0[0], e2[0])

    def step(m):
        amps[odd, m] = product(
            (blocks_h[0, m], blocks_l[0, m]), (pair_h[odd], pair_l[odd]), True) / (pair - col[m] - row)

    each(n, step)


def amps_kernel(weights, e0, e1, e2, e3, vir, far, blocks_h, blocks_l, pair_h, pair_l, amps,
                firsts_h, firsts_l, second_core, traces_in,
                rest_h, rest_l, bars_h, bars_l, crosses, traces, rest_amp, col):
    n = second_core.shape[0]
    odd = is_odd()
    put_split(rest_h.at[1 - odd], rest_l.at[1 - odd], second_core)
    rest_h[odd], rest_l[odd] = pair_h[1], pair_l[1]
    rest_amp[odd] = amps[1]
    col[...] = column(vir[...])
    row = jnp.where(odd == 0, vir[...], far[...])
    pair = e0[0] + jnp.where(odd == 0, e3[0], e1[0])
    pair_first = e0[0] + jnp.where(odd == 0, e2[0], e3[0])
    pair_second = e0[0] + jnp.where(odd == 0, e3[0], e2[0])
    traces[...] = traces_in[...]

    def step(m):
        other = (pair_h[0], pair_l[0])
        sums = col[m] + far[...]
        rest_amp[1 - odd, m] = product(
            (blocks_h[0, m], blocks_l[0, m]), (rest_h[1 - odd], rest_l[1 - odd]), True) / (
                pair - col[m] - row)
        own_amp = amps[0, m]
        bars_h[0, m], bars_l[0, m] = split(float(weights[0]) * own_amp)
        cross = product((blocks_h[1, m], blocks_l[1, m]), other, True) / (e0[0] + e1[0] - sums)
        near_amp = rest_amp[0, m]
        bar = 2.0 * near_amp - cross
        traces[0:1] += lanes(own_amp * own_amp)
        traces[1:2] += lanes(near_amp * bar)
        bars_h[1, m], bars_l[1, m] = split(float(weights[1]) * bar)
        crosses[1 - odd, m] = product((rest_h[1, m], rest_l[1, m]), other, True) / (pair_second - sums)
        crosses[odd, m] = product((firsts_h[odd, m], firsts_l[odd, m]), other, True) / (pair_first - sums)

    each(n, step)
    amp = rest_amp[1]
    bar = 2.0 * amp - amp.T
    traces[pl.ds(3 - odd, 1)] = lanes(amp * bar)
    scale = jnp.where(odd == 0, float(weights[1]), float(weights[2]))
    bars_h[2], bars_l[2] = split(scale * bar)


def add_kernel(terms, before, *refs):
    total = refs[-1]

    def at(ref, slot, m=slice(None)):
        return ref[m] if slot is None else ref[slot, m]

    def step(m):
        value = before[m]
        for k, (bar, block) in enumerate(terms):
            bar_h, bar_l, block_h, block_l = refs[4 * k : 4 * k + 4]
            value += product((at(bar_h, bar, m), at(bar_l, bar, m)), (at(block_h, block), at(block_l, block)), False)
        total[m] = value

    each(before.shape[0], step)


def part_kernel(weights, start, factor, e0, e2, e3, vir, far, blocks_h, blocks_l, two_away, three_away,
                crosses, traces_in, rows_h, rows_l, bar_h, bar_l, traces, col, sums):
    size = two_away.shape[0]
    put_split(rows_h.at[:size], rows_l.at[:size], two_away)
    put_split(rows_h.at[size:], rows_l.at[size:], three_away)
    part = slice(start, start + size)
    col[...] = column(vir[...])
    row = jnp.concatenate([e0[0] + e2[0] - far[:, part], e0[0] + e3[0] - far[:, part]], axis=1)
    lane = lax.broadcasted_iota(jnp.int32, (1, 2 * size), 1)
    scale = jnp.where(lane < size, float(weights[2]), float(weights[1]))
    sums[...] = jnp.zeros(sums.shape, F32)

    def step(m):
        amp = product((blocks_h[0, m], blocks_l[0, m]), (rows_h[...], rows_l[...]), True) / (row - col[m])
        bar = 2.0 * amp - jnp.concatenate([crosses[0, m, part], crosses[1, m, part]], axis=1)
        sums[...] += lanes(amp * bar)
        bar_h[m], bar_l[m] = split(scale * bar)

    each(col.shape[0], step)
    two, three = sums[:, :size], sums[:, size:]
    if factor is None:
        traces[...] = traces_in[...]
        traces[2:3, :size] += two
        traces[3:4, :size] += three
        return
    odd = is_odd()
    whole = [jnp.sum(traces_in[k : k + 1], axis=1, keepdims=True) for k in range(4)]
    whole[2] += jnp.sum(two, axis=1, keepdims=True)
    whole[3] += jnp.sum(three, axis=1, keepdims=True)
    lane = lax.broadcasted_iota(jnp.int32, (1, 128), 1)
    by_offset = [whole[0], jnp.where(odd == 1, whole[1], whole[3]), whole[2]]
    traces[...] = sum(jnp.where(lane == k, by_offset[k], 0.0) for k in range(3)) * factor


VMEM = pl.BlockSpec(memory_space=pltpu.VMEM)
SMEM = pl.BlockSpec(memory_space=pltpu.SMEM)


def call(kernel, units, inputs, outputs, scratch):
    rows = outputs[0][0][-2]
    return pl.pallas_call(
        kernel,
        in_specs=[SMEM if value.size == 1 else VMEM for value in inputs],
        out_specs=tuple(VMEM for _ in outputs),
        out_shape=tuple(jax.ShapeDtypeStruct(*o) for o in outputs),
        scratch_shapes=scratch,
        compiler_params=pltpu.CompilerParams(vmem_limit_bytes=VMEM_LIMIT),
        cost_estimate=pl.CostEstimate(
            flops=units * 6 * rows * rows * 1280, bytes_accessed=8 << 20, transcendentals=0
        ),
    )(*inputs)


def gathered_plane(factor, occ_energy, vir_energy):
    own = factor[0]
    rows, aux = own.shape
    half = rows // 2
    occs = lax.axis_size("occ")

    def core(value):
        return permuted(value, lambda i, v: (i ^ 1, v))

    def mixed(value, parity):
        return permuted(value, lambda i, v: (i ^ 2, v) if i % 2 == parity else (i, v ^ 1))

    far_vir = permuted(vir_energy, lambda i, v: (i, v ^ 1))
    e0 = occ_energy
    e1, e2, e3 = (permuted(e0, lambda i, v, m=m: (i ^ m, v)) for m in (1, 2, 3))
    near = core(own)
    first = mixed(own, 0)
    second = mixed(own, 1)
    first_core = core(first)
    low_first, high_first = first[:half], first[half:]
    low_part = mixed(low_first, 1)
    high_part = mixed(high_first, 1)
    second_core = core(second)
    low_core, high_core = core(low_part), core(high_part)

    weights = [weight(d, occs) for d in range(3)]
    vir, far = vir_energy[None, :], far_vir[None, :]

    block, square = (rows, aux), (rows, rows)
    dense = (block, F32)
    doubles = [((2, *block), BF16)] * 2
    lines = ((8, rows), F32)
    bar = pltpu.VMEM(square, BF16)
    col = pltpu.VMEM((rows, 1), F32)
    amp = pltpu.VMEM(square, F32)
    sums = pltpu.VMEM((1, 2 * half), F32)

    density, *blocks, traces = call(
        functools.partial(start_kernel, weights), 4,
        [e0, e1, vir, own, near], [dense, *doubles, lines], [col, amp, bar, bar])
    density, *firsts, far_amp, traces = call(
        functools.partial(first_kernel, weights), 3,
        [e0, e1, e2, e3, vir, far, *blocks, first, first_core, density, traces],
        [dense, *doubles, (square, F32), lines], [col, amp, bar, bar])
    *pair, amps = call(
        middle_kernel, 1,
        [e0, e2, vir, far, *blocks, *firsts, far_amp, second], [*doubles, ((2, *square), F32)], [col])
    *rest, bars_h, bars_l, crosses, traces = call(
        functools.partial(amps_kernel, weights), 4,
        [e0, e1, e2, e3, vir, far, *blocks, *pair, amps, *firsts, second_core, traces],
        [*doubles, ((3, *square), BF16), ((3, *square), BF16), ((2, *square), F32), lines],
        [pltpu.VMEM((2, *square), F32), col])

    def add(before, *terms):
        slots = tuple((bar_slot, block_slot) for bar_slot, _, block_slot, _ in terms)
        arrays = [array for _, some_bars, _, some_blocks in terms for array in (*some_bars, *some_blocks)]
        return call(
            functools.partial(add_kernel, slots), len(terms), [before, *arrays], [dense], [])[0]

    def part(start, factor, two_away, three_away, traces):
        out = lines if factor is None else ((1, 128), F32)
        *parts, bar_h, bar_l, traces = call(
            functools.partial(part_kernel, weights, start, factor), 1,
            [e0, e2, e3, vir, far, *blocks, two_away, three_away, crosses, traces],
            [((2 * half, aux), BF16)] * 2 + [((rows, 2 * half), BF16)] * 2 + [out], [col, sums])
        return parts, (bar_h, bar_l), traces

    all_bars = (bars_h, bars_l)
    density = add(density, (0, all_bars, 0, pair), (1, all_bars, 0, rest))
    part_0, part_bars_0, traces = part(0, None, low_part, low_core, traces)
    density = add(density, (2, all_bars, 1, rest))
    density = add(density, (None, part_bars_0, None, part_0))
    scale = 1.0 / (rows * lax.axis_size("vir"))
    part_1, part_bars_1, traces = part(half, scale, high_part, high_core, traces)
    density = add(density, (None, part_bars_1, None, part_1))
    return density[None], traces


def contract(pattern, former, latter):
    return jnp.einsum(
        pattern, former, latter, precision=lax.Precision.HIGH, preferred_element_type=F32
    )


def gathered_ring(factor, occ_energy, vir_energy):
    own = factor[0]
    occs = lax.axis_size("occ")
    far_vir = permuted(vir_energy, lambda i, v: (i, v ^ 1))
    own_far = permuted(own, lambda i, v: (i, v ^ 1))
    sums_near = vir_energy[:, None] + vir_energy[None, :]
    sums_far = vir_energy[:, None] + far_vir[None, :]
    density, trace_of = 0.0, {}
    for d in range(occs):
        if weight(d, occs) == 0:
            continue
        near = permuted(own, lambda i, v, d=d: (i - d, v))
        far = permuted(near, lambda i, v: (i, v ^ 1))
        pair = occ_energy[0] + permuted(occ_energy, lambda i, v, d=d: (i - d, v))[0]
        amp_near = contract("ap,bp->ab", own, near) / (pair - sums_near)
        amp_far = contract("ap,bp->ab", own, far) / (pair - sums_far)
        cross = contract("ap,bp->ab", near, own_far) / (pair - sums_far)
        bar_near = 2.0 * amp_near - amp_near.T
        bar_far = 2.0 * amp_far - cross
        density = density + weight(d, occs) * (
            contract("ab,bp->ap", bar_near, near) + contract("ab,bp->ap", bar_far, far)
        )
        trace_of[d] = jnp.sum(amp_near * bar_near) + jnp.sum(amp_far * bar_far)
    return density[None], jnp.stack([trace_of[k % occs] for k in range(STEPS)])


def local(factor, occ_energy, vir_energy):
    gathered = gathered_plane if lax.axis_size("occ") == 4 else gathered_ring
    density, traces = gathered(factor, occ_energy, vir_energy)
    virs = lax.axis_size("vir")
    nvir = factor.shape[1] * virs
    if gathered is gathered_ring:
        return density, lax.psum(traces[None] / nvir, "vir")
    apart = 1
    while apart < virs:
        traces = traces + permuted(traces, lambda i, v: (i, v ^ apart))
        apart *= 2
    return density, traces[:, :STEPS]


def solution(mesh):
    placed = (P("occ", "vir", None), P("occ"), P("vir"))
    return jax.shard_map(
        local,
        mesh=mesh,
        in_specs=placed,
        out_specs=(P("occ", "vir", None), P("occ", None)),
        check_vma=False,
    )
```

profile of v0, /device:TPU:0, one launch (start us, length us, event | category | flops | bytes accessed | tf_op | source)
XLA Modules:
  0.0 154.7 jit_solution(5870826980157434000)
XLA Ops:
  0.6 3.0 %collective-permute-start.5 = (f32[512,1280]{1,0:T(8,128)}, f32[512,1280]{1,0:T(8,128)S(1)}, u32[]{:S(2)}, u32[]{:S(2)}) collective-permute-start(f32[512,1280]{1,0:T(8,128)} %bitcast.16), channel_id=1, source_target_pairs={{16,0},{17,1},{18,2},{19,3},{20,4},{21,5},{22,6},{23,7},{9,8},{8,9... | collective-permute-start | bytes 7864328 | tf_op jit(solution)/shard_map/ppermute | solution.py:24
  3.7 1.5 collective-permute-start.7
  5.2 55.9 %collective-permute-done.5.first = f32[512,1280]{1,0:T(8,128)S(1)} collective-permute-done((f32[512,1280]{1,0:T(8,128)}, f32[512,1280]{1,0:T(8,128)S(1)}, u32[]{:S(2)}, u32[]{:S(2)}) %collective-permute-start.5) | collective-permute-done | bytes 2621472 | tf_op jit(solution)/shard_map/ppermute | solution.py:24
  61.7 2.4 %collective-permute-start.1 = (f32[1]{0:T(128)}, f32[1]{0:T(128)}, u32[]{:S(2)}, u32[]{:S(2)}) collective-permute-start(f32[1]{0:T(128)} %param.4), channel_id=1, source_target_pairs={{16,0},{17,1},{18,2},{19,3},{20,4},{21,5},{22,6},{23,7},{24,8},{25... | collective-permute-start | bytes 20 | tf_op jit(solution)/shard_map/ppermute | solution.py:24
  64.2 2.0 %collective-permute-done.e1 = f32[1]{0:T(128)} collective-permute-done((f32[1]{0:T(128)}, f32[1]{0:T(128)}, u32[]{:S(2)}, u32[]{:S(2)}) %collective-permute-start) | collective-permute-done | bytes 36 | tf_op jit(solution)/shard_map/ppermute | solution.py:24
  66.2 2.1 %collective-permute-start.2 = (f32[1]{0:T(128)}, f32[1]{0:T(128)}, u32[]{:S(2)}, u32[]{:S(2)}) collective-permute-start(f32[1]{0:T(128)} %param.4), channel_id=1, source_target_pairs={{24,0},{25,1},{26,2},{27,3},{28,4},{29,5},{30,6},{31,7},{16,8},{17... | collective-permute-start | bytes 20 | tf_op jit(solution)/shard_map/ppermute | solution.py:24
  69.0 0.8 collective-permute-done.2.e3
  69.8 1.1 collective-permute-start.11
  71.6 1.0 collective-permute-start.3
  72.6 12.5 %shard_map.50 = (f32[512,1280]{1,0:T(8,128)S(1)}, bf16[2,512,1280]{2,1,0:T(8,128)(2,1)S(1)}, bf16[2,512,1280]{2,1,0:T(8,128)(2,1)S(1)}, f32[8,512]{1,0:T(8,128)S(1)}) custom-call(f32[1]{0:T(128)S(6)} %copy.5.e0, f32[1]{0:T(128)} %collective-permute-done.e1, f32[1,512]{1,0:T(1,128)S(1)} %bitcast.5, f32[512,1280]{1,0:T(8,128)S(1)} %bitcast.19, ...), custom_call_target="tpu_custom_call" | custom-call | flops 8053063680 | bytes 8388608 | tf_op jit(solution)/shard_map/pallas_call | solution.py:253
  85.0 0.9 collective-permute-done.9.two_away
  85.9 14.0 %collective-permute-done.11.two_away = f32[256,1280]{1,0:T(8,128)S(1)} collective-permute-done((f32[256,1280]{1,0:T(8,128)S(1)}, f32[256,1280]{1,0:T(8,128)S(1)}, u32[]{:S(2)}, u32[]{:S(2)}) %collective-permute-start.11) | collective-permute-done | bytes 1310752 | tf_op jit(solution)/shard_map/ppermute | solution.py:24
  100.0 10.2 %shard_map.51 = (f32[512,1280]{1,0:T(8,128)S(1)}, bf16[2,512,1280]{2,1,0:T(8,128)(2,1)S(1)}, bf16[2,512,1280]{2,1,0:T(8,128)(2,1)S(1)}, f32[512,512]{1,0:T(8,128)S(1)}, f32[8,512]{1,0:T(8,128)S(1)}) custom-call(f32[1]{0:T(128)S(6)} %copy.5.e0, f32[1]{0:T(128)} %collective-permute-done.e1, f32[1]{0:T(128)} %collective-permute-done.1.e2, ...), custom_call_target="tpu_custom_call" | custom-call | flops 6039797760 | bytes 8388608 | tf_op jit(solution)/shard_map/pallas_call | solution.py:253
  110.2 4.0 %shard_map.52 = (bf16[2,512,1280]{2,1,0:T(8,128)(2,1)S(1)}, bf16[2,512,1280]{2,1,0:T(8,128)(2,1)S(1)}, f32[2,512,512]{2,1,0:T(8,128)S(1)}) custom-call(f32[1]{0:T(128)S(6)} %copy.5.e0, f32[1]{0:T(128)} %collective-permute-done.1.e2, f32[1,512]{1,0:T(1,128)S(1)} %bitcast.7, f32[1,512]{1,0:T(1,128)S(1)} %bitcast.12, ...), custom_call_target="tpu_custom_call" | custom-call | flops 2013265920 | bytes 8388608 | tf_op jit(solution)/shard_map/pallas_call | solution.py:253
  114.2 12.3 %shard_map.53 = (bf16[2,512,1280]{2,1,0:T(8,128)(2,1)S(1)}, bf16[2,512,1280]{2,1,0:T(8,128)(2,1)S(1)}, bf16[3,512,512]{2,1,0:T(8,128)(2,1)S(1)}, bf16[3,512,512]...) custom-call(f32[1]{0:T(128)S(6)} %copy.5.e0, f32[1]{0:T(128)} %collective-permute-done.e1, ...), custom_call_target="tpu_custom_call" | custom-call | flops 8053063680 | bytes 8388608 | tf_op jit(solution)/shard_map/pallas_call | solution.py:253
  126.6 4.7 %shard_map.56 = (bf16[512,1280]{1,0:T(8,128)(2,1)S(1)}, bf16[512,1280]{1,0:T(8,128)(2,1)S(1)}, bf16[512,512]{1,0:T(8,128)(2,1)S(1)}, bf16[512,512]{1,0:T(8,128)(2,1)S(1)}, f32[8,512]{1,0:T(8,128)S(1)}) custom-call(f32[1]{0:T(128)S(6)} %copy.5.e0, f32[1]{0:T(128)} %collective-permute-done.1.e2, f32[1]{0:T(128)} %collective-permute-done.2.e3, ...), custom_call_target="tpu_custom_call" | custom-call | flops 2013265920 | bytes 8388608 | tf_op jit(solution)/shard_map/pallas_call | solution.py:253
  131.3 4.6 %shard_map.58 = (bf16[512,1280]{1,0:T(8,128)(2,1)S(1)}, bf16[512,1280]{1,0:T(8,128)(2,1)S(1)}, bf16[512,512]{1,0:T(8,128)(2,1)S(1)}, bf16[512,512]{1,0:T(8,128)(2,1)S(1)}, f32[1,128]{1,0:T(1,128)S(1)}) custom-call(f32[1]{0:T(128)S(6)} %copy.5.e0, f32[1]{0:T(128)} %collective-permute-done.1.e2, f32[1]{0:T(128)} %collective-permute-done.2.e3, ...), custom_call_target="tpu_custom_call" | custom-call | flops 2013265920 | bytes 8388608 | tf_op jit(solution)/shard_map/pallas_call | solution.py:253
  135.8 0.7 collective-permute-start.13
  136.6 4.5 %shard_map.54.before = f32[512,1280]{1,0:T(8,128)S(1)} custom-call(f32[512,1280]{1,0:T(8,128)S(1)} %get-tuple-element.34.before, bf16[3,512,512]{2,1,0:T(8,128)(2,1)S(1)} %get-tuple-element.42.refs_0_.refs_4_, bf16[3,512,512]{2,1,0:T(8,128)(2,1)S(1)} %get-tuple-element.43.refs_1_.refs_5_, bf16[2,512,1280]{2,1,0:T(8,128)(2,1)S(1)} %get-tuple-element.38.pair_h.refs_2_, ...), custom_call_target="tpu_custom_call" | custom-call | flops 4026531840 | bytes 8388608 | tf_op jit(solution)/shard_map/pallas_call | solution.py:253
  141.1 2.4 %shard_map.55.before = f32[512,1280]{1,0:T(8,128)S(1)} custom-call(f32[512,1280]{1,0:T(8,128)S(1)} %shard_map.54.before, bf16[3,512,512]{2,1,0:T(8,128)(2,1)S(1)} %get-tuple-element.42.refs_0_.refs_4_, bf16[3,512,512]{2,1,0:T(8,128)(2,1)S(1)} %get-tuple-element.43.refs_1_.refs_5_, bf16[2,512,1280]{2,1,0:T(8,128)(2,1)S(1)} %get-tuple-element.44.refs_6_.refs_2_, ...), custom_call_target="tpu_custom_call" | custom-call | flops 2013265920 | bytes 8388608 | tf_op jit(solution)/shard_map/pallas_call | solution.py:253
  143.5 1.6 %collective-permute-start.14 = (f32[1,128]{1,0:T(1,128)S(1)}, f32[1,128]{1,0:T(1,128)S(1)}, u32[]{:S(2)}, u32[]{:S(2)}) collective-permute-start(f32[1,128]{1,0:T(1,128)S(1)} %add.9), channel_id=1, source_target_pairs={{2,0},{3,1},{0,2},{1,3},{6,4},{7,5},{4,6},{5,7},{10,8},{11,9},{8,1... | collective-permute-start | bytes 1544 | tf_op jit(solution)/shard_map/ppermute | solution.py:24
  145.2 2.4 %shard_map.57.before = f32[512,1280]{1,0:T(8,128)S(1)} custom-call(f32[512,1280]{1,0:T(8,128)S(1)} %shard_map.55.before, bf16[512,512]{1,0:T(8,128)(2,1)S(1)} %get-tuple-element.48.refs_0_, bf16[512,512]{1,0:T(8,128)(2,1)S(1)} %get-tuple-element.49.refs_1_, bf16[512,1280]{1,0:T(8,128)(2,1)S(1)} %get-tuple-element.50.refs_2_, ...), custom_call_target="tpu_custom_call" | custom-call | flops 2013265920 | bytes 8388608 | tf_op jit(solution)/shard_map/pallas_call | solution.py:253
  147.6 2.7 %collective-permute-start.15 = (f32[1,128]{1,0:T(1,128)S(1)}, f32[1,128]{1,0:T(1,128)S(1)}, u32[]{:S(2)}, u32[]{:S(2)}) collective-permute-start(f32[1,128]{1,0:T(1,128)S(1)} %add.10), channel_id=1, source_target_pairs={{4,0},{5,1},{6,2},{7,3},{0,4},{1,5},{2,6},{3,7},{12,8},{13,9},{14,... | collective-permute-start | bytes 1544 | tf_op jit(solution)/shard_map/ppermute | solution.py:24
  150.2 3.9 %shard_map.59 = f32[512,1280]{1,0:T(8,128)} custom-call(f32[512,1280]{1,0:T(8,128)S(1)} %shard_map.57.before, bf16[512,512]{1,0:T(8,128)(2,1)S(1)} %get-tuple-element.53.refs_0_, bf16[512,512]{1,0:T(8,128)(2,1)S(1)} %get-tuple-element.54.refs_1_, bf16[512,1280]{1,0:T(8,128)(2,1)S(1)} %get-tuple-element.55.refs_2_, ...), custom_call_target="tpu_custom_call" | custom-call | flops 2013265920 | bytes 8388608 | tf_op jit(solution)/shard_map/pallas_call | solution.py:253
  (26 shorter events, 2.0 us)
Async XLA Ops:
  0.6 70.9 %copy-start = (f32[512]{0:T(512)S(1)}, f32[512]{0:T(512)}, u32[]{:S(2)}) copy-start(f32[512]{0:T(512)} %param.5) | copy-start | bytes 6148
  0.6 71.9 %copy-start.1 = (f32[1,512,1280]{2,1,0:T(8,128)S(1)}, f32[1,512,1280]{2,1,0:T(8,128)}, u32[]{:S(2)}) copy-start(f32[1,512,1280]{2,1,0:T(8,128)} %param.3) | copy-start | bytes 7864324
  0.6 60.5 %collective-permute-start.5 = (f32[512,1280]{1,0:T(8,128)}, f32[512,1280]{1,0:T(8,128)S(1)}, u32[]{:S(2)}, u32[]{:S(2)}) collective-permute-start(f32[512,1280]{1,0:T(8,128)} %bitcast.16), channel_id=1, source_target_pairs={{16,0},{17,1},{18,2},{19,3},{20,4},{21,5},{22,6},{23,7},{9,8},{8,9... | collective-permute-start | bytes 7864328 | tf_op jit(solution)/shard_map/ppermute | solution.py:24
  3.7 60.4 %collective-permute-start.7 = (f32[512,1280]{1,0:T(8,128)}, f32[512,1280]{1,0:T(8,128)S(1)}, u32[]{:S(2)}, u32[]{:S(2)}) collective-permute-start(f32[512,1280]{1,0:T(8,128)} %bitcast.17), channel_id=1, source_target_pairs={{1,0},{0,1},{3,2},{2,3},{5,4},{4,5},{7,6},{6,7},{24,8},{25,9},{26,... | collective-permute-start | bytes 7864328 | tf_op jit(solution)/shard_map/ppermute | solution.py:24
  5.2 66.3 %collective-permute-start.4 = (f32[512,1280]{1,0:T(8,128)}, f32[512,1280]{1,0:T(8,128)S(1)}, u32[]{:S(2)}, u32[]{:S(2)}) collective-permute-start(f32[512,1280]{1,0:T(8,128)} %bitcast.18), channel_id=1, source_target_pairs={{8,0},{9,1},{10,2},{11,3},{12,4},{13,5},{14,6},{15,7},{0,8},{1,9},... | collective-permute-start | bytes 7864328 | tf_op jit(solution)/shard_map/ppermute | solution.py:24
  61.1 38.9 %collective-permute-start.6 = (f32[512,1280]{1,0:T(8,128)S(1)}, f32[512,1280]{1,0:T(8,128)S(1)}, u32[]{:S(2)}, u32[]{:S(2)}) collective-permute-start(f32[512,1280]{1,0:T(8,128)S(1)} %collective-permute-done.5.first), channel_id=1, source_target_pairs={{8,0},{9,1},{10,2},{11,3},{12,4},{13,5},{14,6},{15,7},{0,8},{1,9},... | collective-permute-start | bytes 7864328 | tf_op jit(solution)/shard_map/ppermute | solution.py:24
  61.1 5.0 %collective-permute-start = (f32[1]{0:T(128)}, f32[1]{0:T(128)}, u32[]{:S(2)}, u32[]{:S(2)}) collective-permute-start(f32[1]{0:T(128)} %param.4), channel_id=1, source_target_pairs={{8,0},{9,1},{10,2},{11,3},{12,4},{13,5},{14,6},{15,7},{0,8},{1,9},... | collective-permute-start | bytes 20 | tf_op jit(solution)/shard_map/ppermute | solution.py:24
  61.7 6.7 %collective-permute-start.1 = (f32[1]{0:T(128)}, f32[1]{0:T(128)}, u32[]{:S(2)}, u32[]{:S(2)}) collective-permute-start(f32[1]{0:T(128)} %param.4), channel_id=1, source_target_pairs={{16,0},{17,1},{18,2},{19,3},{20,4},{21,5},{22,6},{23,7},{24,8},{25... | collective-permute-start | bytes 20 | tf_op jit(solution)/shard_map/ppermute | solution.py:24
  64.0 50.2 %collective-permute-start.8 = (f32[512,1280]{1,0:T(8,128)S(1)}, f32[512,1280]{1,0:T(8,128)S(1)}, u32[]{:S(2)}, u32[]{:S(2)}) collective-permute-start(f32[512,1280]{1,0:T(8,128)S(1)} %collective-permute-done.7.second), channel_id=1, source_target_pairs={{8,0},{9,1},{10,2},{11,3},{12,4},{13,5},{14,6},{15,7},{0,8},{1,9},... | collective-permute-start | bytes 7864328 | tf_op jit(solution)/shard_map/ppermute | solution.py:24
  66.2 3.6 %collective-permute-start.2 = (f32[1]{0:T(128)}, f32[1]{0:T(128)}, u32[]{:S(2)}, u32[]{:S(2)}) collective-permute-start(f32[1]{0:T(128)} %param.4), channel_id=1, source_target_pairs={{24,0},{25,1},{26,2},{27,3},{28,4},{29,5},{30,6},{31,7},{16,8},{17... | collective-permute-start | bytes 20 | tf_op jit(solution)/shard_map/ppermute | solution.py:24
  68.3 17.6 %collective-permute-start.9 = (f32[256,1280]{1,0:T(8,128)S(1)}, f32[256,1280]{1,0:T(8,128)S(1)}, u32[]{:S(2)}, u32[]{:S(2)}) collective-permute-start(f32[256,1280]{1,0:T(8,128)S(1)} %get-tuple-element.59), channel_id=1, source_target_pairs={{1,0},{0,1},{3,2},{2,3},{5,4},{4,5},{7,6},{6,7},{24,8},{25,9},{26,... | collective-permute-start | bytes 3932168 | tf_op jit(solution)/shard_map/ppermute | solution.py:24
  69.8 30.2 %collective-permute-start.11 = (f32[256,1280]{1,0:T(8,128)S(1)}, f32[256,1280]{1,0:T(8,128)S(1)}, u32[]{:S(2)}, u32[]{:S(2)}) collective-permute-start(f32[256,1280]{1,0:T(8,128)S(1)} %get-tuple-element.58), channel_id=1, source_target_pairs={{1,0},{0,1},{3,2},{2,3},{5,4},{4,5},{7,6},{6,7},{24,8},{25,9},{26,... | collective-permute-start | bytes 3932168 | tf_op jit(solution)/shard_map/ppermute | solution.py:24
  71.6 28.5 %collective-permute-start.3 = (f32[512]{0:T(512)S(1)}, f32[512]{0:T(512)S(1)}, u32[]{:S(2)}, u32[]{:S(2)}) collective-permute-start(f32[512]{0:T(512)S(1)} %copy-done), channel_id=1, source_target_pairs={{1,0},{0,1},{3,2},{2,3},{5,4},{4,5},{7,6},{6,7},{9,8},{8,9},{11,10... | collective-permute-start | bytes 6152 | tf_op jit(solution)/shard_map/ppermute | solution.py:24
  85.9 40.6 %collective-permute-start.10 = (f32[256,1280]{1,0:T(8,128)S(1)}, f32[256,1280]{1,0:T(8,128)S(1)}, u32[]{:S(2)}, u32[]{:S(2)}) collective-permute-start(f32[256,1280]{1,0:T(8,128)S(1)} %collective-permute-done.9.two_away), channel_id=1, source_target_pairs={{8,0},{9,1},{10,2},{11,3},{12,4},{13,5},{14,6},{15,7},{0,8},{1,9},... | collective-permute-start | bytes 3932168 | tf_op jit(solution)/shard_map/ppermute | solution.py:24
  100.0 31.3 %collective-permute-start.12 = (f32[256,1280]{1,0:T(8,128)S(1)}, f32[256,1280]{1,0:T(8,128)S(1)}, u32[]{:S(2)}, u32[]{:S(2)}) collective-permute-start(f32[256,1280]{1,0:T(8,128)S(1)} %collective-permute-done.11.two_away), channel_id=1, source_target_pairs={{8,0},{9,1},{10,2},{11,3},{12,4},{13,5},{14,6},{15,7},{0,8},{1,9},... | collective-permute-start | bytes 3932168 | tf_op jit(solution)/shard_map/ppermute | solution.py:24
  135.8 7.7 %collective-permute-start.13 = (f32[1,128]{1,0:T(1,128)S(1)}, f32[1,128]{1,0:T(1,128)S(1)}, u32[]{:S(2)}, u32[]{:S(2)}) collective-permute-start(f32[1,128]{1,0:T(1,128)S(1)} %get-tuple-element.57), channel_id=1, source_target_pairs={{1,0},{0,1},{3,2},{2,3},{5,4},{4,5},{7,6},{6,7},{9,8},{8,9},{11,10... | collective-permute-start | bytes 1544 | tf_op jit(solution)/shard_map/ppermute | solution.py:24
  143.5 4.0 %collective-permute-start.14 = (f32[1,128]{1,0:T(1,128)S(1)}, f32[1,128]{1,0:T(1,128)S(1)}, u32[]{:S(2)}, u32[]{:S(2)}) collective-permute-start(f32[1,128]{1,0:T(1,128)S(1)} %add.9), channel_id=1, source_target_pairs={{2,0},{3,1},{0,2},{1,3},{6,4},{7,5},{4,6},{5,7},{10,8},{11,9},{8,1... | collective-permute-start | bytes 1544 | tf_op jit(solution)/shard_map/ppermute | solution.py:24
  147.6 6.6 %collective-permute-start.15 = (f32[1,128]{1,0:T(1,128)S(1)}, f32[1,128]{1,0:T(1,128)S(1)}, u32[]{:S(2)}, u32[]{:S(2)}) collective-permute-start(f32[1,128]{1,0:T(1,128)S(1)} %add.10), channel_id=1, source_target_pairs={{4,0},{5,1},{6,2},{7,3},{0,4},{1,5},{2,6},{3,7},{12,8},{13,9},{14,... | collective-permute-start | bytes 1544 | tf_op jit(solution)/shard_map/ppermute | solution.py:24
where the time goes:
time: 155 us
  waiting for transfers between devices  73.7 us (48%)
  Pallas kernels  61.4 us (40%)
  starting transfers between devices  17.4 us (11%)
    ppermute x16, waiting for transfers between devices, permuted(): return lax.ppermute(value, AXES, route)  73.7 us
    pallas_call x10, Pallas kernels, call(): pl.pallas_call(kernel, in_specs=[SMEM if value.size == 1 else VMEM for va...  61.4 us
    ppermute x16, starting transfers between devices, permuted(): return lax.ppermute(value, AXES, route)  17.4 us
  transfers between devices with their start and end apart: 16, of which 5 were waited for; matrix products, arithmetic and copies ran while one was open for 0% of the time, Pallas kernels for 37%

commit v1 on v0

--- a/solution.py
+++ b/solution.py
@@ -197,14 +197,13 @@
 def add_kernel(terms, before, *refs):
     total = refs[-1]
 
-    def at(ref, slot, m=slice(None)):
-        return ref[m] if slot is None else ref[slot, m]
-
     def step(m):
         value = before[m]
-        for k, (bar, block) in enumerate(terms):
+        for k, (bar, block, span) in enumerate(terms):
             bar_h, bar_l, block_h, block_l = refs[4 * k : 4 * k + 4]
-            value += product((at(bar_h, bar, m), at(bar_l, bar, m)), (at(block_h, block), at(block_l, block)), False)
+            left = tuple(ref[m, span] if bar is None else ref[bar, m, span] for ref in (bar_h, bar_l))
+            right = tuple(ref[span] if block is None else ref[block, span] for ref in (block_h, block_l))
+            value += product(left, right, False)
         total[m] = value
 
     each(before.shape[0], step)
@@ -316,8 +315,8 @@
         [*doubles, ((3, *square), BF16), ((3, *square), BF16), ((2, *square), F32), lines],
         [pltpu.VMEM((2, *square), F32), col])
 
-    def add(before, *terms):
-        slots = tuple((bar_slot, block_slot) for bar_slot, _, block_slot, _ in terms)
+    def add(before, *terms, span=slice(None)):
+        slots = tuple((bar_slot, block_slot, span) for bar_slot, _, block_slot, _ in terms)
         arrays = [array for _, some_bars, _, some_blocks in terms for array in (*some_bars, *some_blocks)]
         return call(
             functools.partial(add_kernel, slots), len(terms), [before, *arrays], [dense], [])[0]
@@ -337,7 +336,8 @@
     density = add(density, (None, part_bars_0, None, part_0))
     scale = 1.0 / (rows * lax.axis_size("vir"))
     part_1, part_bars_1, traces = part(half, scale, high_part, high_core, traces)
-    density = add(density, (None, part_bars_1, None, part_1))
+    density = add(density, (None, part_bars_1, None, part_1), span=slice(0, half))
+    density = add(density, (None, part_bars_1, None, part_1), span=slice(half, 2 * half))
     return density[None], traces
 
 

time: 155 us -> 156 us (level)
    pallas_call x10 -> x11, Pallas kernels: 61.4 us -> 61.7 us  [call(): pl.pallas_call(kernel, in_specs=[SMEM if value.size == 1 else VMEM for va...]
  transfers between devices with their start and end apart: 16 -> 16, of which waited for: 5 -> 7; matrix products, arithmetic and copies ran while one was open for 0% -> 0% of each run, Pallas kernels for 37% -> 37%
where the time goes in v1:
time: 156 us
  waiting for transfers between devices  74.7 us (48%)
  Pallas kernels  61.7 us (40%)
  starting transfers between devices  17.3 us (11%)
    ppermute x16, waiting for transfers between devices, permuted(): return lax.ppermute(value, AXES, route)  74.7 us
    pallas_call x11, Pallas kernels, call(): pl.pallas_call(kernel, in_specs=[SMEM if value.size == 1 else VMEM for va...  61.7 us
    ppermute x16, starting transfers between devices, permuted(): return lax.ppermute(value, AXES, route)  17.3 us
  transfers between devices with their start and end apart: 16, of which 7 were waited for; matrix products, arithmetic and copies ran while one was open for 0% of the time, Pallas kernels for 37%

profile of v1, /device:TPU:0, one launch (start us, length us, event | category | flops | bytes accessed | tf_op | source)
XLA Modules:
  0.0 155.9 jit_solution(2409750342949312223)
XLA Ops:
  0.6 3.0 %collective-permute-start.5 = (f32[512,1280]{1,0:T(8,128)}, f32[512,1280]{1,0:T(8,128)S(1)}, u32[]{:S(2)}, u32[]{:S(2)}) collective-permute-start(f32[512,1280]{1,0:T(8,128)} %bitcast.16), channel_id=1, source_target_pairs={{16,0},{17,1},{18,2},{19,3},{20,4},{21,5},{22,6},{23,7},{9,8},{8,9... | collective-permute-start | bytes 7864328 | tf_op jit(solution)/shard_map/ppermute | solution.py:24
  3.7 1.5 collective-permute-start.7
  5.2 55.9 %collective-permute-done.5.first = f32[512,1280]{1,0:T(8,128)S(1)} collective-permute-done((f32[512,1280]{1,0:T(8,128)}, f32[512,1280]{1,0:T(8,128)S(1)}, u32[]{:S(2)}, u32[]{:S(2)}) %collective-permute-start.5) | collective-permute-done | bytes 2621472 | tf_op jit(solution)/shard_map/ppermute | solution.py:24
  61.7 2.4 %collective-permute-start.1 = (f32[1]{0:T(128)}, f32[1]{0:T(128)}, u32[]{:S(2)}, u32[]{:S(2)}) collective-permute-start(f32[1]{0:T(128)} %param.4), channel_id=1, source_target_pairs={{16,0},{17,1},{18,2},{19,3},{20,4},{21,5},{22,6},{23,7},{24,8},{25... | collective-permute-start | bytes 20 | tf_op jit(solution)/shard_map/ppermute | solution.py:24
  64.2 2.0 %collective-permute-done.e1 = f32[1]{0:T(128)} collective-permute-done((f32[1]{0:T(128)}, f32[1]{0:T(128)}, u32[]{:S(2)}, u32[]{:S(2)}) %collective-permute-start) | collective-permute-done | bytes 36 | tf_op jit(solution)/shard_map/ppermute | solution.py:24
  66.2 2.1 %collective-permute-start.2 = (f32[1]{0:T(128)}, f32[1]{0:T(128)}, u32[]{:S(2)}, u32[]{:S(2)}) collective-permute-start(f32[1]{0:T(128)} %param.4), channel_id=1, source_target_pairs={{24,0},{25,1},{26,2},{27,3},{28,4},{29,5},{30,6},{31,7},{16,8},{17... | collective-permute-start | bytes 20 | tf_op jit(solution)/shard_map/ppermute | solution.py:24
  69.0 0.8 collective-permute-done.2.e3
  69.8 1.1 collective-permute-start.11
  71.6 1.0 collective-permute-start.3
  72.6 12.5 %shard_map.50 = (f32[512,1280]{1,0:T(8,128)S(1)}, bf16[2,512,1280]{2,1,0:T(8,128)(2,1)S(1)}, bf16[2,512,1280]{2,1,0:T(8,128)(2,1)S(1)}, f32[8,512]{1,0:T(8,128)S(1)}) custom-call(f32[1]{0:T(128)S(6)} %copy.5.e0, f32[1]{0:T(128)} %collective-permute-done.e1, f32[1,512]{1,0:T(1,128)S(1)} %bitcast.5, f32[512,1280]{1,0:T(8,128)S(1)} %bitcast.19, ...), custom_call_target="tpu_custom_call" | custom-call | flops 8053063680 | bytes 8388608 | tf_op jit(solution)/shard_map/pallas_call | solution.py:252
  85.0 0.9 collective-permute-done.9.two_away
  85.9 14.0 %collective-permute-done.11.two_away = f32[256,1280]{1,0:T(8,128)S(1)} collective-permute-done((f32[256,1280]{1,0:T(8,128)S(1)}, f32[256,1280]{1,0:T(8,128)S(1)}, u32[]{:S(2)}, u32[]{:S(2)}) %collective-permute-start.11) | collective-permute-done | bytes 1310752 | tf_op jit(solution)/shard_map/ppermute | solution.py:24
  100.0 10.2 %shard_map.51 = (f32[512,1280]{1,0:T(8,128)S(1)}, bf16[2,512,1280]{2,1,0:T(8,128)(2,1)S(1)}, bf16[2,512,1280]{2,1,0:T(8,128)(2,1)S(1)}, f32[512,512]{1,0:T(8,128)S(1)}, f32[8,512]{1,0:T(8,128)S(1)}) custom-call(f32[1]{0:T(128)S(6)} %copy.5.e0, f32[1]{0:T(128)} %collective-permute-done.e1, f32[1]{0:T(128)} %collective-permute-done.1.e2, ...), custom_call_target="tpu_custom_call" | custom-call | flops 6039797760 | bytes 8388608 | tf_op jit(solution)/shard_map/pallas_call | solution.py:252
  110.2 4.0 %shard_map.52 = (bf16[2,512,1280]{2,1,0:T(8,128)(2,1)S(1)}, bf16[2,512,1280]{2,1,0:T(8,128)(2,1)S(1)}, f32[2,512,512]{2,1,0:T(8,128)S(1)}) custom-call(f32[1]{0:T(128)S(6)} %copy.5.e0, f32[1]{0:T(128)} %collective-permute-done.1.e2, f32[1,512]{1,0:T(1,128)S(1)} %bitcast.7, f32[1,512]{1,0:T(1,128)S(1)} %bitcast.12, ...), custom_call_target="tpu_custom_call" | custom-call | flops 2013265920 | bytes 8388608 | tf_op jit(solution)/shard_map/pallas_call | solution.py:252
  114.2 12.3 %shard_map.53 = (bf16[2,512,1280]{2,1,0:T(8,128)(2,1)S(1)}, bf16[2,512,1280]{2,1,0:T(8,128)(2,1)S(1)}, bf16[3,512,512]{2,1,0:T(8,128)(2,1)S(1)}, bf16[3,512,512]...) custom-call(f32[1]{0:T(128)S(6)} %copy.5.e0, f32[1]{0:T(128)} %collective-permute-done.e1, ...), custom_call_target="tpu_custom_call" | custom-call | flops 8053063680 | bytes 8388608 | tf_op jit(solution)/shard_map/pallas_call | solution.py:252
  126.5 4.7 %shard_map.54.before = f32[512,1280]{1,0:T(8,128)S(1)} custom-call(f32[512,1280]{1,0:T(8,128)S(1)} %get-tuple-element.34.before, bf16[3,512,512]{2,1,0:T(8,128)(2,1)S(1)} %get-tuple-element.42.refs_0_.refs_4_, bf16[3,512,512]{2,1,0:T(8,128)(2,1)S(1)} %get-tuple-element.43.refs_1_.refs_5_, bf16[2,512,1280]{2,1,0:T(8,128)(2,1)S(1)} %get-tuple-element.38.pair_h.refs_2_, ...), custom_call_target="tpu_custom_call" | custom-call | flops 4026531840 | bytes 8388608 | tf_op jit(solution)/shard_map/pallas_call | solution.py:252
  131.2 2.4 %shard_map.55.before = f32[512,1280]{1,0:T(8,128)S(1)} custom-call(f32[512,1280]{1,0:T(8,128)S(1)} %shard_map.54.before, bf16[3,512,512]{2,1,0:T(8,128)(2,1)S(1)} %get-tuple-element.42.refs_0_.refs_4_, bf16[3,512,512]{2,1,0:T(8,128)(2,1)S(1)} %get-tuple-element.43.refs_1_.refs_5_, bf16[2,512,1280]{2,1,0:T(8,128)(2,1)S(1)} %get-tuple-element.44.refs_6_.refs_2_, ...), custom_call_target="tpu_custom_call" | custom-call | flops 2013265920 | bytes 8388608 | tf_op jit(solution)/shard_map/pallas_call | solution.py:252
  133.6 4.5 %shard_map.56 = (bf16[512,1280]{1,0:T(8,128)(2,1)S(1)}, bf16[512,1280]{1,0:T(8,128)(2,1)S(1)}, bf16[512,512]{1,0:T(8,128)(2,1)S(1)}, bf16[512,512]{1,0:T(8,128)(2,1)S(1)}, f32[8,512]{1,0:T(8,128)S(1)}) custom-call(f32[1]{0:T(128)S(6)} %copy.5.e0, f32[1]{0:T(128)} %collective-permute-done.1.e2, f32[1]{0:T(128)} %collective-permute-done.2.e3, ...), custom_call_target="tpu_custom_call" | custom-call | flops 2013265920 | bytes 8388608 | tf_op jit(solution)/shard_map/pallas_call | solution.py:252
  138.2 4.6 %shard_map.58 = (bf16[512,1280]{1,0:T(8,128)(2,1)S(1)}, bf16[512,1280]{1,0:T(8,128)(2,1)S(1)}, bf16[512,512]{1,0:T(8,128)(2,1)S(1)}, bf16[512,512]{1,0:T(8,128)(2,1)S(1)}, f32[1,128]{1,0:T(1,128)S(1)}) custom-call(f32[1]{0:T(128)S(6)} %copy.5.e0, f32[1]{0:T(128)} %collective-permute-done.1.e2, f32[1]{0:T(128)} %collective-permute-done.2.e3, ...), custom_call_target="tpu_custom_call" | custom-call | flops 2013265920 | bytes 8388608 | tf_op jit(solution)/shard_map/pallas_call | solution.py:252
  143.5 2.4 %shard_map.57.before = f32[512,1280]{1,0:T(8,128)S(1)} custom-call(f32[512,1280]{1,0:T(8,128)S(1)} %shard_map.55.before, bf16[512,512]{1,0:T(8,128)(2,1)S(1)} %get-tuple-element.48.refs_0_, bf16[512,512]{1,0:T(8,128)(2,1)S(1)} %get-tuple-element.49.refs_1_, bf16[512,1280]{1,0:T(8,128)(2,1)S(1)} %get-tuple-element.50.refs_2_, ...), custom_call_target="tpu_custom_call" | custom-call | flops 2013265920 | bytes 8388608 | tf_op jit(solution)/shard_map/pallas_call | solution.py:252
  146.3 1.6 %collective-permute-start.14 = (f32[1,128]{1,0:T(1,128)S(1)}, f32[1,128]{1,0:T(1,128)S(1)}, u32[]{:S(2)}, u32[]{:S(2)}) collective-permute-start(f32[1,128]{1,0:T(1,128)S(1)} %add.9), channel_id=1, source_target_pairs={{2,0},{3,1},{0,2},{1,3},{6,4},{7,5},{4,6},{5,7},{10,8},{11,9},{8,1... | collective-permute-start | bytes 1544 | tf_op jit(solution)/shard_map/ppermute | solution.py:24
  147.9 1.4 shard_map.59.before
  149.9 2.6 %collective-permute-start.15 = (f32[1,128]{1,0:T(1,128)S(1)}, f32[1,128]{1,0:T(1,128)S(1)}, u32[]{:S(2)}, u32[]{:S(2)}) collective-permute-start(f32[1,128]{1,0:T(1,128)S(1)} %add.10), channel_id=1, source_target_pairs={{4,0},{5,1},{6,2},{7,3},{0,4},{1,5},{2,6},{3,7},{12,8},{13,9},{14,... | collective-permute-start | bytes 1544 | tf_op jit(solution)/shard_map/ppermute | solution.py:24
  152.5 2.9 %shard_map.60 = f32[512,1280]{1,0:T(8,128)} custom-call(f32[512,1280]{1,0:T(8,128)S(1)} %shard_map.59.before, bf16[512,512]{1,0:T(8,128)(2,1)S(1)} %get-tuple-element.53.refs_0_, bf16[512,512]{1,0:T(8,128)(2,1)S(1)} %get-tuple-element.54.refs_1_, bf16[512,1280]{1,0:T(8,128)(2,1)S(1)} %get-tuple-element.55.refs_2_, ...), custom_call_target="tpu_custom_call" | custom-call | flops 2013265920 | bytes 8388608 | tf_op jit(solution)/shard_map/pallas_call | solution.py:252
  (27 shorter events, 3.8 us)
Async XLA Ops:
  0.6 70.9 %copy-start = (f32[512]{0:T(512)S(1)}, f32[512]{0:T(512)}, u32[]{:S(2)}) copy-start(f32[512]{0:T(512)} %param.5) | copy-start | bytes 6148
  0.6 71.9 %copy-start.1 = (f32[1,512,1280]{2,1,0:T(8,128)S(1)}, f32[1,512,1280]{2,1,0:T(8,128)}, u32[]{:S(2)}) copy-start(f32[1,512,1280]{2,1,0:T(8,128)} %param.3) | copy-start | bytes 7864324
  0.6 60.5 %collective-permute-start.5 = (f32[512,1280]{1,0:T(8,128)}, f32[512,1280]{1,0:T(8,128)S(1)}, u32[]{:S(2)}, u32[]{:S(2)}) collective-permute-start(f32[512,1280]{1,0:T(8,128)} %bitcast.16), channel_id=1, source_target_pairs={{16,0},{17,1},{18,2},{19,3},{20,4},{21,5},{22,6},{23,7},{9,8},{8,9... | collective-permute-start | bytes 7864328 | tf_op jit(solution)/shard_map/ppermute | solution.py:24
  3.7 60.4 %collective-permute-start.7 = (f32[512,1280]{1,0:T(8,128)}, f32[512,1280]{1,0:T(8,128)S(1)}, u32[]{:S(2)}, u32[]{:S(2)}) collective-permute-start(f32[512,1280]{1,0:T(8,128)} %bitcast.17), channel_id=1, source_target_pairs={{1,0},{0,1},{3,2},{2,3},{5,4},{4,5},{7,6},{6,7},{24,8},{25,9},{26,... | collective-permute-start | bytes 7864328 | tf_op jit(solution)/shard_map/ppermute | solution.py:24
  5.2 66.3 %collective-permute-start.4 = (f32[512,1280]{1,0:T(8,128)}, f32[512,1280]{1,0:T(8,128)S(1)}, u32[]{:S(2)}, u32[]{:S(2)}) collective-permute-start(f32[512,1280]{1,0:T(8,128)} %bitcast.18), channel_id=1, source_target_pairs={{8,0},{9,1},{10,2},{11,3},{12,4},{13,5},{14,6},{15,7},{0,8},{1,9},... | collective-permute-start | bytes 7864328 | tf_op jit(solution)/shard_map/ppermute | solution.py:24
  61.1 38.9 %collective-permute-start.6 = (f32[512,1280]{1,0:T(8,128)S(1)}, f32[512,1280]{1,0:T(8,128)S(1)}, u32[]{:S(2)}, u32[]{:S(2)}) collective-permute-start(f32[512,1280]{1,0:T(8,128)S(1)} %collective-permute-done.5.first), channel_id=1, source_target_pairs={{8,0},{9,1},{10,2},{11,3},{12,4},{13,5},{14,6},{15,7},{0,8},{1,9},... | collective-permute-start | bytes 7864328 | tf_op jit(solution)/shard_map/ppermute | solution.py:24
  61.1 5.0 %collective-permute-start = (f32[1]{0:T(128)}, f32[1]{0:T(128)}, u32[]{:S(2)}, u32[]{:S(2)}) collective-permute-start(f32[1]{0:T(128)} %param.4), channel_id=1, source_target_pairs={{8,0},{9,1},{10,2},{11,3},{12,4},{13,5},{14,6},{15,7},{0,8},{1,9},... | collective-permute-start | bytes 20 | tf_op jit(solution)/shard_map/ppermute | solution.py:24
  61.7 6.7 %collective-permute-start.1 = (f32[1]{0:T(128)}, f32[1]{0:T(128)}, u32[]{:S(2)}, u32[]{:S(2)}) collective-permute-start(f32[1]{0:T(128)} %param.4), channel_id=1, source_target_pairs={{16,0},{17,1},{18,2},{19,3},{20,4},{21,5},{22,6},{23,7},{24,8},{25... | collective-permute-start | bytes 20 | tf_op jit(solution)/shard_map/ppermute | solution.py:24
  64.0 50.2 %collective-permute-start.8 = (f32[512,1280]{1,0:T(8,128)S(1)}, f32[512,1280]{1,0:T(8,128)S(1)}, u32[]{:S(2)}, u32[]{:S(2)}) collective-permute-start(f32[512,1280]{1,0:T(8,128)S(1)} %collective-permute-done.7.second), channel_id=1, source_target_pairs={{8,0},{9,1},{10,2},{11,3},{12,4},{13,5},{14,6},{15,7},{0,8},{1,9},... | collective-permute-start | bytes 7864328 | tf_op jit(solution)/shard_map/ppermute | solution.py:24
  66.2 3.6 %collective-permute-start.2 = (f32[1]{0:T(128)}, f32[1]{0:T(128)}, u32[]{:S(2)}, u32[]{:S(2)}) collective-permute-start(f32[1]{0:T(128)} %param.4), channel_id=1, source_target_pairs={{24,0},{25,1},{26,2},{27,3},{28,4},{29,5},{30,6},{31,7},{16,8},{17... | collective-permute-start | bytes 20 | tf_op jit(solution)/shard_map/ppermute | solution.py:24
  68.3 17.6 %collective-permute-start.9 = (f32[256,1280]{1,0:T(8,128)S(1)}, f32[256,1280]{1,0:T(8,128)S(1)}, u32[]{:S(2)}, u32[]{:S(2)}) collective-permute-start(f32[256,1280]{1,0:T(8,128)S(1)} %get-tuple-element.59), channel_id=1, source_target_pairs={{1,0},{0,1},{3,2},{2,3},{5,4},{4,5},{7,6},{6,7},{24,8},{25,9},{26,... | collective-permute-start | bytes 3932168 | tf_op jit(solution)/shard_map/ppermute | solution.py:24
  69.8 30.2 %collective-permute-start.11 = (f32[256,1280]{1,0:T(8,128)S(1)}, f32[256,1280]{1,0:T(8,128)S(1)}, u32[]{:S(2)}, u32[]{:S(2)}) collective-permute-start(f32[256,1280]{1,0:T(8,128)S(1)} %get-tuple-element.58), channel_id=1, source_target_pairs={{1,0},{0,1},{3,2},{2,3},{5,4},{4,5},{7,6},{6,7},{24,8},{25,9},{26,... | collective-permute-start | bytes 3932168 | tf_op jit(solution)/shard_map/ppermute | solution.py:24
  71.6 28.5 %collective-permute-start.3 = (f32[512]{0:T(512)S(1)}, f32[512]{0:T(512)S(1)}, u32[]{:S(2)}, u32[]{:S(2)}) collective-permute-start(f32[512]{0:T(512)S(1)} %copy-done), channel_id=1, source_target_pairs={{1,0},{0,1},{3,2},{2,3},{5,4},{4,5},{7,6},{6,7},{9,8},{8,9},{11,10... | collective-permute-start | bytes 6152 | tf_op jit(solution)/shard_map/ppermute | solution.py:24
  85.9 47.7 %collective-permute-start.10 = (f32[256,1280]{1,0:T(8,128)S(1)}, f32[256,1280]{1,0:T(8,128)S(1)}, u32[]{:S(2)}, u32[]{:S(2)}) collective-permute-start(f32[256,1280]{1,0:T(8,128)S(1)} %collective-permute-done.9.two_away), channel_id=1, source_target_pairs={{8,0},{9,1},{10,2},{11,3},{12,4},{13,5},{14,6},{15,7},{0,8},{1,9},... | collective-permute-start | bytes 3932168 | tf_op jit(solution)/shard_map/ppermute | solution.py:24
  100.0 38.2 %collective-permute-start.12 = (f32[256,1280]{1,0:T(8,128)S(1)}, f32[256,1280]{1,0:T(8,128)S(1)}, u32[]{:S(2)}, u32[]{:S(2)}) collective-permute-start(f32[256,1280]{1,0:T(8,128)S(1)} %collective-permute-done.11.two_away), channel_id=1, source_target_pairs={{8,0},{9,1},{10,2},{11,3},{12,4},{13,5},{14,6},{15,7},{0,8},{1,9},... | collective-permute-start | bytes 3932168 | tf_op jit(solution)/shard_map/ppermute | solution.py:24
  142.7 3.6 %collective-permute-start.13 = (f32[1,128]{1,0:T(1,128)S(1)}, f32[1,128]{1,0:T(1,128)S(1)}, u32[]{:S(2)}, u32[]{:S(2)}) collective-permute-start(f32[1,128]{1,0:T(1,128)S(1)} %get-tuple-element.57), channel_id=1, source_target_pairs={{1,0},{0,1},{3,2},{2,3},{5,4},{4,5},{7,6},{6,7},{9,8},{8,9},{11,10... | collective-permute-start | bytes 1544 | tf_op jit(solution)/shard_map/ppermute | solution.py:24
  146.3 3.6 %collective-permute-start.14 = (f32[1,128]{1,0:T(1,128)S(1)}, f32[1,128]{1,0:T(1,128)S(1)}, u32[]{:S(2)}, u32[]{:S(2)}) collective-permute-start(f32[1,128]{1,0:T(1,128)S(1)} %add.9), channel_id=1, source_target_pairs={{2,0},{3,1},{0,2},{1,3},{6,4},{7,5},{4,6},{5,7},{10,8},{11,9},{8,1... | collective-permute-start | bytes 1544 | tf_op jit(solution)/shard_map/ppermute | solution.py:24
  149.9 5.5 %collective-permute-start.15 = (f32[1,128]{1,0:T(1,128)S(1)}, f32[1,128]{1,0:T(1,128)S(1)}, u32[]{:S(2)}, u32[]{:S(2)}) collective-permute-start(f32[1,128]{1,0:T(1,128)S(1)} %add.10), channel_id=1, source_target_pairs={{4,0},{5,1},{6,2},{7,3},{0,4},{1,5},{2,6},{3,7},{12,8},{13,9},{14,... | collective-permute-start | bytes 1544 | tf_op jit(solution)/shard_map/ppermute | solution.py:24

commit v2 on v1

--- a/solution.py
+++ b/solution.py
@@ -60,6 +60,9 @@
 
 
 def each(rows, body, count=2):
+    if count == 1:
+        body(slice(None))
+        return
     size = rows // count
 
     def step(m, carry):
@@ -151,7 +154,7 @@
         amps[odd, m] = product(
             (blocks_h[0, m], blocks_l[0, m]), (pair_h[odd], pair_l[odd]), True) / (pair - col[m] - row)
 
-    each(n, step)
+    each(n, step, 1)
 
 
 def amps_kernel(weights, e0, e1, e2, e3, vir, far, blocks_h, blocks_l, pair_h, pair_l, amps,
@@ -186,7 +189,7 @@
         crosses[1 - odd, m] = product((rest_h[1, m], rest_l[1, m]), other, True) / (pair_second - sums)
         crosses[odd, m] = product((firsts_h[odd, m], firsts_l[odd, m]), other, True) / (pair_first - sums)
 
-    each(n, step)
+    each(n, step, 1)
     amp = rest_amp[1]
     bar = 2.0 * amp - amp.T
     traces[pl.ds(3 - odd, 1)] = lanes(amp * bar)
@@ -206,7 +209,7 @@
             value += product(left, right, False)
         total[m] = value
 
-    each(before.shape[0], step)
+    each(before.shape[0], step, 1)
 
 
 def part_kernel(weights, start, factor, e0, e2, e3, vir, far, blocks_h, blocks_l, two_away, three_away,
@@ -227,7 +230,7 @@
         sums[...] += lanes(amp * bar)
         bar_h[m], bar_l[m] = split(scale * bar)
 
-    each(col.shape[0], step)
+    each(col.shape[0], step, 1)
     two, three = sums[:, :size], sums[:, size:]
     if factor is None:
         traces[...] = traces_in[...]

time: 156 us -> 155 us (level)
  Pallas kernels: 61.7 us -> 60 us
    pallas_call x11, Pallas kernels: 61.7 us -> 60 us  [call(): pl.pallas_call(kernel, in_specs=[SMEM if value.size == 1 else VMEM for va...]
  transfers between devices with their start and end apart: 16 -> 16, of which waited for: 7 -> 7; matrix products, arithmetic and copies ran while one was open for 0% -> 0% of each run, Pallas kernels for 37% -> 36%
where the time goes in v2:
time: 155 us; the launch traced here: 154 us
  waiting for transfers between devices  75.1 us (48%)
  Pallas kernels  60 us (39%)
  starting transfers between devices  17.3 us (11%)
    ppermute x16, waiting for transfers between devices, permuted(): return lax.ppermute(value, AXES, route)  75.1 us
    pallas_call x11, Pallas kernels, call(): pl.pallas_call(kernel, in_specs=[SMEM if value.size == 1 else VMEM for va...  60 us
    ppermute x16, starting transfers between devices, permuted(): return lax.ppermute(value, AXES, route)  17.3 us
  transfers between devices with their start and end apart: 16, of which 7 were waited for; matrix products, arithmetic and copies ran while one was open for 0% of the time, Pallas kernels for 36%

profile of v2, /device:TPU:0, one launch (start us, length us, event | category | flops | bytes accessed | tf_op | source)
XLA Modules:
  0.0 154.5 jit_solution(13258234753475852896)
XLA Ops:
  0.6 3.0 %collective-permute-start.5 = (f32[512,1280]{1,0:T(8,128)}, f32[512,1280]{1,0:T(8,128)S(1)}, u32[]{:S(2)}, u32[]{:S(2)}) collective-permute-start(f32[512,1280]{1,0:T(8,128)} %bitcast.16), channel_id=1, source_target_pairs={{16,0},{17,1},{18,2},{19,3},{20,4},{21,5},{22,6},{23,7},{9,8},{8,9... | collective-permute-start | bytes 7864328 | tf_op jit(solution)/shard_map/ppermute | solution.py:24
  3.7 1.5 collective-permute-start.7
  5.2 55.9 %collective-permute-done.5.first = f32[512,1280]{1,0:T(8,128)S(1)} collective-permute-done((f32[512,1280]{1,0:T(8,128)}, f32[512,1280]{1,0:T(8,128)S(1)}, u32[]{:S(2)}, u32[]{:S(2)}) %collective-permute-start.5) | collective-permute-done | bytes 2621472 | tf_op jit(solution)/shard_map/ppermute | solution.py:24
  61.7 2.4 %collective-permute-start.1 = (f32[1]{0:T(128)}, f32[1]{0:T(128)}, u32[]{:S(2)}, u32[]{:S(2)}) collective-permute-start(f32[1]{0:T(128)} %param.4), channel_id=1, source_target_pairs={{16,0},{17,1},{18,2},{19,3},{20,4},{21,5},{22,6},{23,7},{24,8},{25... | collective-permute-start | bytes 20 | tf_op jit(solution)/shard_map/ppermute | solution.py:24
  64.2 2.0 %collective-permute-done.e1 = f32[1]{0:T(128)} collective-permute-done((f32[1]{0:T(128)}, f32[1]{0:T(128)}, u32[]{:S(2)}, u32[]{:S(2)}) %collective-permute-start) | collective-permute-done | bytes 36 | tf_op jit(solution)/shard_map/ppermute | solution.py:24
  66.2 2.1 %collective-permute-start.2 = (f32[1]{0:T(128)}, f32[1]{0:T(128)}, u32[]{:S(2)}, u32[]{:S(2)}) collective-permute-start(f32[1]{0:T(128)} %param.4), channel_id=1, source_target_pairs={{24,0},{25,1},{26,2},{27,3},{28,4},{29,5},{30,6},{31,7},{16,8},{17... | collective-permute-start | bytes 20 | tf_op jit(solution)/shard_map/ppermute | solution.py:24
  69.8 1.1 collective-permute-start.11
  71.6 1.0 collective-permute-start.3
  72.6 12.5 %shard_map.50 = (f32[512,1280]{1,0:T(8,128)S(1)}, bf16[2,512,1280]{2,1,0:T(8,128)(2,1)S(1)}, bf16[2,512,1280]{2,1,0:T(8,128)(2,1)S(1)}, f32[8,512]{1,0:T(8,128)S(1)}) custom-call(f32[1]{0:T(128)S(6)} %copy.5.e0, f32[1]{0:T(128)} %collective-permute-done.e1, f32[1,512]{1,0:T(1,128)S(1)} %bitcast.5, f32[512,1280]{1,0:T(8,128)S(1)} %bitcast.19, ...), custom_call_target="tpu_custom_call" | custom-call | flops 8053063680 | bytes 8388608 | tf_op jit(solution)/shard_map/pallas_call | solution.py:255
  85.0 0.9 collective-permute-done.9.two_away
  85.9 14.0 %collective-permute-done.11.two_away = f32[256,1280]{1,0:T(8,128)S(1)} collective-permute-done((f32[256,1280]{1,0:T(8,128)S(1)}, f32[256,1280]{1,0:T(8,128)S(1)}, u32[]{:S(2)}, u32[]{:S(2)}) %collective-permute-start.11) | collective-permute-done | bytes 1310752 | tf_op jit(solution)/shard_map/ppermute | solution.py:24
  100.0 10.2 %shard_map.51 = (f32[512,1280]{1,0:T(8,128)S(1)}, bf16[2,512,1280]{2,1,0:T(8,128)(2,1)S(1)}, bf16[2,512,1280]{2,1,0:T(8,128)(2,1)S(1)}, f32[512,512]{1,0:T(8,128)S(1)}, f32[8,512]{1,0:T(8,128)S(1)}) custom-call(f32[1]{0:T(128)S(6)} %copy.5.e0, f32[1]{0:T(128)} %collective-permute-done.e1, f32[1]{0:T(128)} %collective-permute-done.1.e2, ...), custom_call_target="tpu_custom_call" | custom-call | flops 6039797760 | bytes 8388608 | tf_op jit(solution)/shard_map/pallas_call | solution.py:255
  110.2 3.5 %shard_map.52 = (bf16[2,512,1280]{2,1,0:T(8,128)(2,1)S(1)}, bf16[2,512,1280]{2,1,0:T(8,128)(2,1)S(1)}, f32[2,512,512]{2,1,0:T(8,128)S(1)}) custom-call(f32[1]{0:T(128)S(6)} %copy.5.e0, f32[1]{0:T(128)} %collective-permute-done.1.e2, f32[1,512]{1,0:T(1,128)S(1)} %bitcast.7, f32[1,512]{1,0:T(1,128)S(1)} %bitcast.12, ...), custom_call_target="tpu_custom_call" | custom-call | flops 2013265920 | bytes 8388608 | tf_op jit(solution)/shard_map/pallas_call | solution.py:255
  113.7 12.3 %shard_map.53 = (bf16[2,512,1280]{2,1,0:T(8,128)(2,1)S(1)}, bf16[2,512,1280]{2,1,0:T(8,128)(2,1)S(1)}, bf16[3,512,512]{2,1,0:T(8,128)(2,1)S(1)}, bf16[3,512,512]...) custom-call(f32[1]{0:T(128)S(6)} %copy.5.e0, f32[1]{0:T(128)} %collective-permute-done.e1, ...), custom_call_target="tpu_custom_call" | custom-call | flops 8053063680 | bytes 8388608 | tf_op jit(solution)/shard_map/pallas_call | solution.py:255
  126.0 4.4 %shard_map.54.before = f32[512,1280]{1,0:T(8,128)S(1)} custom-call(f32[512,1280]{1,0:T(8,128)S(1)} %get-tuple-element.34.before, bf16[3,512,512]{2,1,0:T(8,128)(2,1)S(1)} %get-tuple-element.42.refs_0_.refs_4_, bf16[3,512,512]{2,1,0:T(8,128)(2,1)S(1)} %get-tuple-element.43.refs_1_.refs_5_, bf16[2,512,1280]{2,1,0:T(8,128)(2,1)S(1)} %get-tuple-element.38.pair_h.refs_2_, ...), custom_call_target="tpu_custom_call" | custom-call | flops 4026531840 | bytes 8388608 | tf_op jit(solution)/shard_map/pallas_call | solution.py:255
  130.4 2.3 %shard_map.55.before = f32[512,1280]{1,0:T(8,128)S(1)} custom-call(f32[512,1280]{1,0:T(8,128)S(1)} %shard_map.54.before, bf16[3,512,512]{2,1,0:T(8,128)(2,1)S(1)} %get-tuple-element.42.refs_0_.refs_4_, bf16[3,512,512]{2,1,0:T(8,128)(2,1)S(1)} %get-tuple-element.43.refs_1_.refs_5_, bf16[2,512,1280]{2,1,0:T(8,128)(2,1)S(1)} %get-tuple-element.44.refs_6_.refs_2_, ...), custom_call_target="tpu_custom_call" | custom-call | flops 2013265920 | bytes 8388608 | tf_op jit(solution)/shard_map/pallas_call | solution.py:255
  132.7 4.5 %shard_map.56 = (bf16[512,1280]{1,0:T(8,128)(2,1)S(1)}, bf16[512,1280]{1,0:T(8,128)(2,1)S(1)}, bf16[512,512]{1,0:T(8,128)(2,1)S(1)}, bf16[512,512]{1,0:T(8,128)(2,1)S(1)}, f32[8,512]{1,0:T(8,128)S(1)}) custom-call(f32[1]{0:T(128)S(6)} %copy.5.e0, f32[1]{0:T(128)} %collective-permute-done.1.e2, f32[1]{0:T(128)} %collective-permute-done.2.e3, ...), custom_call_target="tpu_custom_call" | custom-call | flops 2013265920 | bytes 8388608 | tf_op jit(solution)/shard_map/pallas_call | solution.py:255
  137.2 4.3 %shard_map.58 = (bf16[512,1280]{1,0:T(8,128)(2,1)S(1)}, bf16[512,1280]{1,0:T(8,128)(2,1)S(1)}, bf16[512,512]{1,0:T(8,128)(2,1)S(1)}, bf16[512,512]{1,0:T(8,128)(2,1)S(1)}, f32[1,128]{1,0:T(1,128)S(1)}) custom-call(f32[1]{0:T(128)S(6)} %copy.5.e0, f32[1]{0:T(128)} %collective-permute-done.1.e2, f32[1]{0:T(128)} %collective-permute-done.2.e3, ...), custom_call_target="tpu_custom_call" | custom-call | flops 2013265920 | bytes 8388608 | tf_op jit(solution)/shard_map/pallas_call | solution.py:255
  142.3 2.2 %shard_map.57.before = f32[512,1280]{1,0:T(8,128)S(1)} custom-call(f32[512,1280]{1,0:T(8,128)S(1)} %shard_map.55.before, bf16[512,512]{1,0:T(8,128)(2,1)S(1)} %get-tuple-element.48.refs_0_, bf16[512,512]{1,0:T(8,128)(2,1)S(1)} %get-tuple-element.49.refs_1_, bf16[512,1280]{1,0:T(8,128)(2,1)S(1)} %get-tuple-element.50.refs_2_, ...), custom_call_target="tpu_custom_call" | custom-call | flops 2013265920 | bytes 8388608 | tf_op jit(solution)/shard_map/pallas_call | solution.py:255
  145.1 1.6 %collective-permute-start.14 = (f32[1,128]{1,0:T(1,128)S(1)}, f32[1,128]{1,0:T(1,128)S(1)}, u32[]{:S(2)}, u32[]{:S(2)}) collective-permute-start(f32[1,128]{1,0:T(1,128)S(1)} %add.9), channel_id=1, source_target_pairs={{2,0},{3,1},{0,2},{1,3},{6,4},{7,5},{4,6},{5,7},{10,8},{11,9},{8,1... | collective-permute-start | bytes 1544 | tf_op jit(solution)/shard_map/ppermute | solution.py:24
  146.7 1.2 shard_map.59.before
  147.9 0.8 collective-permute-done.14
  148.7 2.6 %collective-permute-start.15 = (f32[1,128]{1,0:T(1,128)S(1)}, f32[1,128]{1,0:T(1,128)S(1)}, u32[]{:S(2)}, u32[]{:S(2)}) collective-permute-start(f32[1,128]{1,0:T(1,128)S(1)} %add.10), channel_id=1, source_target_pairs={{4,0},{5,1},{6,2},{7,3},{0,4},{1,5},{2,6},{3,7},{12,8},{13,9},{14,... | collective-permute-start | bytes 1544 | tf_op jit(solution)/shard_map/ppermute | solution.py:24
  151.3 2.7 %shard_map.60 = f32[512,1280]{1,0:T(8,128)} custom-call(f32[512,1280]{1,0:T(8,128)S(1)} %shard_map.59.before, bf16[512,512]{1,0:T(8,128)(2,1)S(1)} %get-tuple-element.53.refs_0_, bf16[512,512]{1,0:T(8,128)(2,1)S(1)} %get-tuple-element.54.refs_1_, bf16[512,1280]{1,0:T(8,128)(2,1)S(1)} %get-tuple-element.55.refs_2_, ...), custom_call_target="tpu_custom_call" | custom-call | flops 2013265920 | bytes 8388608 | tf_op jit(solution)/shard_map/pallas_call | solution.py:255
  (27 shorter events, 4.1 us)
Async XLA Ops:
  0.6 70.9 %copy-start = (f32[512]{0:T(512)S(1)}, f32[512]{0:T(512)}, u32[]{:S(2)}) copy-start(f32[512]{0:T(512)} %param.5) | copy-start | bytes 6148
  0.6 71.9 %copy-start.1 = (f32[1,512,1280]{2,1,0:T(8,128)S(1)}, f32[1,512,1280]{2,1,0:T(8,128)}, u32[]{:S(2)}) copy-start(f32[1,512,1280]{2,1,0:T(8,128)} %param.3) | copy-start | bytes 7864324
  0.6 60.5 %collective-permute-start.5 = (f32[512,1280]{1,0:T(8,128)}, f32[512,1280]{1,0:T(8,128)S(1)}, u32[]{:S(2)}, u32[]{:S(2)}) collective-permute-start(f32[512,1280]{1,0:T(8,128)} %bitcast.16), channel_id=1, source_target_pairs={{16,0},{17,1},{18,2},{19,3},{20,4},{21,5},{22,6},{23,7},{9,8},{8,9... | collective-permute-start | bytes 7864328 | tf_op jit(solution)/shard_map/ppermute | solution.py:24
  3.7 60.4 %collective-permute-start.7 = (f32[512,1280]{1,0:T(8,128)}, f32[512,1280]{1,0:T(8,128)S(1)}, u32[]{:S(2)}, u32[]{:S(2)}) collective-permute-start(f32[512,1280]{1,0:T(8,128)} %bitcast.17), channel_id=1, source_target_pairs={{1,0},{0,1},{3,2},{2,3},{5,4},{4,5},{7,6},{6,7},{24,8},{25,9},{26,... | collective-permute-start | bytes 7864328 | tf_op jit(solution)/shard_map/ppermute | solution.py:24
  5.2 66.3 %collective-permute-start.4 = (f32[512,1280]{1,0:T(8,128)}, f32[512,1280]{1,0:T(8,128)S(1)}, u32[]{:S(2)}, u32[]{:S(2)}) collective-permute-start(f32[512,1280]{1,0:T(8,128)} %bitcast.18), channel_id=1, source_target_pairs={{8,0},{9,1},{10,2},{11,3},{12,4},{13,5},{14,6},{15,7},{0,8},{1,9},... | collective-permute-start | bytes 7864328 | tf_op jit(solution)/shard_map/ppermute | solution.py:24
  61.1 38.9 %collective-permute-start.6 = (f32[512,1280]{1,0:T(8,128)S(1)}, f32[512,1280]{1,0:T(8,128)S(1)}, u32[]{:S(2)}, u32[]{:S(2)}) collective-permute-start(f32[512,1280]{1,0:T(8,128)S(1)} %collective-permute-done.5.first), channel_id=1, source_target_pairs={{8,0},{9,1},{10,2},{11,3},{12,4},{13,5},{14,6},{15,7},{0,8},{1,9},... | collective-permute-start | bytes 7864328 | tf_op jit(solution)/shard_map/ppermute | solution.py:24
  61.1 5.0 %collective-permute-start = (f32[1]{0:T(128)}, f32[1]{0:T(128)}, u32[]{:S(2)}, u32[]{:S(2)}) collective-permute-start(f32[1]{0:T(128)} %param.4), channel_id=1, source_target_pairs={{8,0},{9,1},{10,2},{11,3},{12,4},{13,5},{14,6},{15,7},{0,8},{1,9},... | collective-permute-start | bytes 20 | tf_op jit(solution)/shard_map/ppermute | solution.py:24
  61.7 6.7 %collective-permute-start.1 = (f32[1]{0:T(128)}, f32[1]{0:T(128)}, u32[]{:S(2)}, u32[]{:S(2)}) collective-permute-start(f32[1]{0:T(128)} %param.4), channel_id=1, source_target_pairs={{16,0},{17,1},{18,2},{19,3},{20,4},{21,5},{22,6},{23,7},{24,8},{25... | collective-permute-start | bytes 20 | tf_op jit(solution)/shard_map/ppermute | solution.py:24
  64.0 49.7 %collective-permute-start.8 = (f32[512,1280]{1,0:T(8,128)S(1)}, f32[512,1280]{1,0:T(8,128)S(1)}, u32[]{:S(2)}, u32[]{:S(2)}) collective-permute-start(f32[512,1280]{1,0:T(8,128)S(1)} %collective-permute-done.7.second), channel_id=1, source_target_pairs={{8,0},{9,1},{10,2},{11,3},{12,4},{13,5},{14,6},{15,7},{0,8},{1,9},... | collective-permute-start | bytes 7864328 | tf_op jit(solution)/shard_map/ppermute | solution.py:24
  66.2 3.6 %collective-permute-start.2 = (f32[1]{0:T(128)}, f32[1]{0:T(128)}, u32[]{:S(2)}, u32[]{:S(2)}) collective-permute-start(f32[1]{0:T(128)} %param.4), channel_id=1, source_target_pairs={{24,0},{25,1},{26,2},{27,3},{28,4},{29,5},{30,6},{31,7},{16,8},{17... | collective-permute-start | bytes 20 | tf_op jit(solution)/shard_map/ppermute | solution.py:24
  68.3 17.6 %collective-permute-start.9 = (f32[256,1280]{1,0:T(8,128)S(1)}, f32[256,1280]{1,0:T(8,128)S(1)}, u32[]{:S(2)}, u32[]{:S(2)}) collective-permute-start(f32[256,1280]{1,0:T(8,128)S(1)} %get-tuple-element.59), channel_id=1, source_target_pairs={{1,0},{0,1},{3,2},{2,3},{5,4},{4,5},{7,6},{6,7},{24,8},{25,9},{26,... | collective-permute-start | bytes 3932168 | tf_op jit(solution)/shard_map/ppermute | solution.py:24
  69.8 30.2 %collective-permute-start.11 = (f32[256,1280]{1,0:T(8,128)S(1)}, f32[256,1280]{1,0:T(8,128)S(1)}, u32[]{:S(2)}, u32[]{:S(2)}) collective-permute-start(f32[256,1280]{1,0:T(8,128)S(1)} %get-tuple-element.58), channel_id=1, source_target_pairs={{1,0},{0,1},{3,2},{2,3},{5,4},{4,5},{7,6},{6,7},{24,8},{25,9},{26,... | collective-permute-start | bytes 3932168 | tf_op jit(solution)/shard_map/ppermute | solution.py:24
  71.6 28.5 %collective-permute-start.3 = (f32[512]{0:T(512)S(1)}, f32[512]{0:T(512)S(1)}, u32[]{:S(2)}, u32[]{:S(2)}) collective-permute-start(f32[512]{0:T(512)S(1)} %copy-done), channel_id=1, source_target_pairs={{1,0},{0,1},{3,2},{2,3},{5,4},{4,5},{7,6},{6,7},{9,8},{8,9},{11,10... | collective-permute-start | bytes 6152 | tf_op jit(solution)/shard_map/ppermute | solution.py:24
  85.9 46.7 %collective-permute-start.10 = (f32[256,1280]{1,0:T(8,128)S(1)}, f32[256,1280]{1,0:T(8,128)S(1)}, u32[]{:S(2)}, u32[]{:S(2)}) collective-permute-start(f32[256,1280]{1,0:T(8,128)S(1)} %collective-permute-done.9.two_away), channel_id=1, source_target_pairs={{8,0},{9,1},{10,2},{11,3},{12,4},{13,5},{14,6},{15,7},{0,8},{1,9},... | collective-permute-start | bytes 3932168 | tf_op jit(solution)/shard_map/ppermute | solution.py:24
  100.0 37.2 %collective-permute-start.12 = (f32[256,1280]{1,0:T(8,128)S(1)}, f32[256,1280]{1,0:T(8,128)S(1)}, u32[]{:S(2)}, u32[]{:S(2)}) collective-permute-start(f32[256,1280]{1,0:T(8,128)S(1)} %collective-permute-done.11.two_away), channel_id=1, source_target_pairs={{8,0},{9,1},{10,2},{11,3},{12,4},{13,5},{14,6},{15,7},{0,8},{1,9},... | collective-permute-start | bytes 3932168 | tf_op jit(solution)/shard_map/ppermute | solution.py:24
  141.5 3.6 %collective-permute-start.13 = (f32[1,128]{1,0:T(1,128)S(1)}, f32[1,128]{1,0:T(1,128)S(1)}, u32[]{:S(2)}, u32[]{:S(2)}) collective-permute-start(f32[1,128]{1,0:T(1,128)S(1)} %get-tuple-element.57), channel_id=1, source_target_pairs={{1,0},{0,1},{3,2},{2,3},{5,4},{4,5},{7,6},{6,7},{9,8},{8,9},{11,10... | collective-permute-start | bytes 1544 | tf_op jit(solution)/shard_map/ppermute | solution.py:24
  145.1 3.6 %collective-permute-start.14 = (f32[1,128]{1,0:T(1,128)S(1)}, f32[1,128]{1,0:T(1,128)S(1)}, u32[]{:S(2)}, u32[]{:S(2)}) collective-permute-start(f32[1,128]{1,0:T(1,128)S(1)} %add.9), channel_id=1, source_target_pairs={{2,0},{3,1},{0,2},{1,3},{6,4},{7,5},{4,6},{5,7},{10,8},{11,9},{8,1... | collective-permute-start | bytes 1544 | tf_op jit(solution)/shard_map/ppermute | solution.py:24
  148.7 5.3 %collective-permute-start.15 = (f32[1,128]{1,0:T(1,128)S(1)}, f32[1,128]{1,0:T(1,128)S(1)}, u32[]{:S(2)}, u32[]{:S(2)}) collective-permute-start(f32[1,128]{1,0:T(1,128)S(1)} %add.10), channel_id=1, source_target_pairs={{4,0},{5,1},{6,2},{7,3},{0,4},{1,5},{2,6},{3,7},{12,8},{13,9},{14,... | collective-permute-start | bytes 1544 | tf_op jit(solution)/shard_map/ppermute | solution.py:24

commit v3 on v2

--- a/solution.py
+++ b/solution.py
@@ -79,22 +79,23 @@
     each(rows.shape[0], step, 4)
 
 
-def start_kernel(weights, e0, e1, vir, own, near, total, blocks_h, blocks_l, traces,
-                 col, amp, bar_h, bar_l):
+def start_kernel(weights, e0, e1, vir, own, near, total, blocks_h, blocks_l, traces, col,
+                 amp, bar_h, bar_l):
     n = own.shape[0]
     put_split(blocks_h.at[0], blocks_l.at[0], own)
     put_split(blocks_h.at[1], blocks_l.at[1], near)
     total[...] = jnp.zeros(total.shape, F32)
     traces[...] = jnp.zeros(traces.shape, F32)
+    col[...] = column(vir[...])
 
     def block(k, carry):
         pair = e0[0] + jnp.where(k == 0, e0[0], e1[0])
         scale = jnp.where(k == 0, float(weights[0]), float(weights[1]))
-        col[...] = pair - column(vir[...])
+        row = pair - vir[...]
 
         def amps(m):
             amp[m] = product((blocks_h[0, m], blocks_l[0, m]), (blocks_h[k], blocks_l[k]), True) / (
-                col[m] - vir[...])
+                row - col[m])
 
         each(n, amps)
         bar = 2.0 * amp[...] - amp[...].T
@@ -111,21 +112,21 @@
 
 
 def first_kernel(weights, e0, e1, e2, e3, vir, far, blocks_h, blocks_l, first, first_core, before,
-                 traces_in, total, firsts_h, firsts_l, far_amp, traces, col, amp, bar_h, bar_l):
+                 traces_in, col, total, firsts_h, firsts_l, far_amp, traces, rows, amp, bar_h, bar_l):
     n = first.shape[0]
     odd = is_odd()
     put_split(firsts_h.at[0], firsts_l.at[0], first)
     put_split(firsts_h.at[1], firsts_l.at[1], first_core)
-    pair = e0[0] + jnp.where(odd == 0, e2[0], e3[0])
-    pair_far = e0[0] + jnp.where(odd == 0, e1[0], e0[0])
     scale = jnp.where(odd == 0, float(weights[2]), float(weights[1]))
-    col[...] = column(vir[...])
+    for k, other in enumerate((e0, e1, e2, e3)):
+        rows[k : k + 1] = e0[0] + other[0] - far[...]
+        rows[k + 4 : k + 5] = e0[0] + other[0] - vir[...]
+    row, row_far = rows[pl.ds(6 + odd, 1)], rows[pl.ds(1 - odd, 1)]
 
     def amps(m):
         left = (blocks_h[0, m], blocks_l[0, m])
-        amp[m] = product(left, (firsts_h[odd], firsts_l[odd]), True) / (pair - col[m] - vir[...])
-        far_amp[m] = product(left, (firsts_h[1 - odd], firsts_l[1 - odd]), True) / (
-            pair_far - col[m] - far[...])
+        amp[m] = product(left, (firsts_h[odd], firsts_l[odd]), True) / (row - col[m])
+        far_amp[m] = product(left, (firsts_h[1 - odd], firsts_l[1 - odd]), True) / (row_far - col[m])
 
     each(n, amps)
     bar = 2.0 * amp[...] - amp[...].T
@@ -139,55 +140,48 @@
     each(n, totals)
 
 
-def middle_kernel(e0, e2, vir, far, blocks_h, blocks_l, firsts_h, firsts_l, far_amp, second,
-                  pair_h, pair_l, amps, col):
+def middle_kernel(rows, col, blocks_h, blocks_l, firsts_h, firsts_l, far_amp, second,
+                  pair_h, pair_l, amps):
     n = second.shape[0]
     odd = is_odd()
     put_split(pair_h.at[odd], pair_l.at[odd], second)
     pair_h[1 - odd], pair_l[1 - odd] = firsts_h[1 - odd], firsts_l[1 - odd]
     amps[1 - odd] = far_amp[...]
-    col[...] = column(vir[...])
-    row = jnp.where(odd == 0, far[...], vir[...])
-    pair = e0[0] + jnp.where(odd == 0, e0[0], e2[0])
+    row = rows[pl.ds(6 * odd, 1)]
 
     def step(m):
         amps[odd, m] = product(
-            (blocks_h[0, m], blocks_l[0, m]), (pair_h[odd], pair_l[odd]), True) / (pair - col[m] - row)
+            (blocks_h[0, m], blocks_l[0, m]), (pair_h[odd], pair_l[odd]), True) / (row - col[m])
 
     each(n, step, 1)
 
 
-def amps_kernel(weights, e0, e1, e2, e3, vir, far, blocks_h, blocks_l, pair_h, pair_l, amps,
+def amps_kernel(weights, rows, col, blocks_h, blocks_l, pair_h, pair_l, amps,
                 firsts_h, firsts_l, second_core, traces_in,
-                rest_h, rest_l, bars_h, bars_l, crosses, traces, rest_amp, col):
+                rest_h, rest_l, bars_h, bars_l, crosses, traces, rest_amp):
     n = second_core.shape[0]
     odd = is_odd()
     put_split(rest_h.at[1 - odd], rest_l.at[1 - odd], second_core)
     rest_h[odd], rest_l[odd] = pair_h[1], pair_l[1]
     rest_amp[odd] = amps[1]
-    col[...] = column(vir[...])
-    row = jnp.where(odd == 0, vir[...], far[...])
-    pair = e0[0] + jnp.where(odd == 0, e3[0], e1[0])
-    pair_first = e0[0] + jnp.where(odd == 0, e2[0], e3[0])
-    pair_second = e0[0] + jnp.where(odd == 0, e3[0], e2[0])
+    row = rows[pl.ds(7 - 6 * odd, 1)]
+    row_first, row_second = rows[pl.ds(2 + odd, 1)], rows[pl.ds(3 - odd, 1)]
     traces[...] = traces_in[...]
 
     def step(m):
         other = (pair_h[0], pair_l[0])
-        sums = col[m] + far[...]
         rest_amp[1 - odd, m] = product(
-            (blocks_h[0, m], blocks_l[0, m]), (rest_h[1 - odd], rest_l[1 - odd]), True) / (
-                pair - col[m] - row)
+            (blocks_h[0, m], blocks_l[0, m]), (rest_h[1 - odd], rest_l[1 - odd]), True) / (row - col[m])
         own_amp = amps[0, m]
         bars_h[0, m], bars_l[0, m] = split(float(weights[0]) * own_amp)
-        cross = product((blocks_h[1, m], blocks_l[1, m]), other, True) / (e0[0] + e1[0] - sums)
+        cross = product((blocks_h[1, m], blocks_l[1, m]), other, True) / (rows[1:2] - col[m])
         near_amp = rest_amp[0, m]
         bar = 2.0 * near_amp - cross
         traces[0:1] += lanes(own_amp * own_amp)
         traces[1:2] += lanes(near_amp * bar)
         bars_h[1, m], bars_l[1, m] = split(float(weights[1]) * bar)
-        crosses[1 - odd, m] = product((rest_h[1, m], rest_l[1, m]), other, True) / (pair_second - sums)
-        crosses[odd, m] = product((firsts_h[odd, m], firsts_l[odd, m]), other, True) / (pair_first - sums)
+        crosses[1 - odd, m] = product((rest_h[1, m], rest_l[1, m]), other, True) / (row_second - col[m])
+        crosses[odd, m] = product((firsts_h[odd, m], firsts_l[odd, m]), other, True) / (row_first - col[m])
 
     each(n, step, 1)
     amp = rest_amp[1]
@@ -212,14 +206,13 @@
     each(before.shape[0], step, 1)
 
 
-def part_kernel(weights, start, factor, e0, e2, e3, vir, far, blocks_h, blocks_l, two_away, three_away,
-                crosses, traces_in, rows_h, rows_l, bar_h, bar_l, traces, col, sums):
+def part_kernel(weights, start, factor, rows, col, blocks_h, blocks_l, two_away, three_away,
+                crosses, traces_in, rows_h, rows_l, bar_h, bar_l, traces, sums):
     size = two_away.shape[0]
     put_split(rows_h.at[:size], rows_l.at[:size], two_away)
     put_split(rows_h.at[size:], rows_l.at[size:], three_away)
     part = slice(start, start + size)
-    col[...] = column(vir[...])
-    row = jnp.concatenate([e0[0] + e2[0] - far[:, part], e0[0] + e3[0] - far[:, part]], axis=1)
+    row = jnp.concatenate([rows[2:3, part], rows[3:4, part]], axis=1)
     lane = lax.broadcasted_iota(jnp.int32, (1, 2 * size), 1)
     scale = jnp.where(lane < size, float(weights[2]), float(weights[1]))
     sums[...] = jnp.zeros(sums.shape, F32)
@@ -298,25 +291,25 @@
     doubles = [((2, *block), BF16)] * 2
     lines = ((8, rows), F32)
     bar = pltpu.VMEM(square, BF16)
-    col = pltpu.VMEM((rows, 1), F32)
+    column_out = ((rows, 1), F32)
     amp = pltpu.VMEM(square, F32)
     sums = pltpu.VMEM((1, 2 * half), F32)
 
-    density, *blocks, traces = call(
+    density, *blocks, traces, col = call(
         functools.partial(start_kernel, weights), 4,
-        [e0, e1, vir, own, near], [dense, *doubles, lines], [col, amp, bar, bar])
-    density, *firsts, far_amp, traces = call(
+        [e0, e1, vir, own, near], [dense, *doubles, lines, column_out], [amp, bar, bar])
+    density, *firsts, far_amp, traces, gap_rows = call(
         functools.partial(first_kernel, weights), 3,
-        [e0, e1, e2, e3, vir, far, *blocks, first, first_core, density, traces],
-        [dense, *doubles, (square, F32), lines], [col, amp, bar, bar])
+        [e0, e1, e2, e3, vir, far, *blocks, first, first_core, density, traces, col],
+        [dense, *doubles, (square, F32), lines, lines], [amp, bar, bar])
     *pair, amps = call(
         middle_kernel, 1,
-        [e0, e2, vir, far, *blocks, *firsts, far_amp, second], [*doubles, ((2, *square), F32)], [col])
+        [gap_rows, col, *blocks, *firsts, far_amp, second], [*doubles, ((2, *square), F32)], [])
     *rest, bars_h, bars_l, crosses, traces = call(
         functools.partial(amps_kernel, weights), 4,
-        [e0, e1, e2, e3, vir, far, *blocks, *pair, amps, *firsts, second_core, traces],
+        [gap_rows, col, *blocks, *pair, amps, *firsts, second_core, traces],
         [*doubles, ((3, *square), BF16), ((3, *square), BF16), ((2, *square), F32), lines],
-        [pltpu.VMEM((2, *square), F32), col])
+        [pltpu.VMEM((2, *square), F32)])
 
     def add(before, *terms, span=slice(None)):
         slots = tuple((bar_slot, block_slot, span) for bar_slot, _, block_slot, _ in terms)
@@ -328,8 +321,8 @@
         out = lines if factor is None else ((1, 128), F32)
         *parts, bar_h, bar_l, traces = call(
             functools.partial(part_kernel, weights, start, factor), 1,
-            [e0, e2, e3, vir, far, *blocks, two_away, three_away, crosses, traces],
-            [((2 * half, aux), BF16)] * 2 + [((rows, 2 * half), BF16)] * 2 + [out], [col, sums])
+            [gap_rows, col, *blocks, two_away, three_away, crosses, traces],
+            [((2 * half, aux), BF16)] * 2 + [((rows, 2 * half), BF16)] * 2 + [out], [sums])
         return parts, (bar_h, bar_l), traces
 
     all_bars = (bars_h, bars_l)

time: 155 us -> 149 us (0.961)
  Pallas kernels: 60 us -> 54 us
    pallas_call x11, Pallas kernels: 60 us -> 54 us  [call(): pl.pallas_call(kernel, in_specs=[SMEM if value.size == 1 else VMEM for va...]
  transfers between devices with their start and end apart: 16 -> 16, of which waited for: 7 -> 7; matrix products, arithmetic and copies ran while one was open for 0% -> 0% of each run, Pallas kernels for 36% -> 34%
where the time goes in v3:
time: 149 us
  waiting for transfers between devices  75.3 us (51%)
  Pallas kernels  54 us (36%)
  starting transfers between devices  17.3 us (12%)
    ppermute x16, waiting for transfers between devices, permuted(): return lax.ppermute(value, AXES, route)  75.3 us
    pallas_call x11, Pallas kernels, call(): pl.pallas_call(kernel, in_specs=[SMEM if value.size == 1 else VMEM for va...  54 us
    ppermute x16, starting transfers between devices, permuted(): return lax.ppermute(value, AXES, route)  17.3 us
  transfers between devices with their start and end apart: 16, of which 7 were waited for; matrix products, arithmetic and copies ran while one was open for 0% of the time, Pallas kernels for 34%

profile of v3, /device:TPU:0, one launch (start us, length us, event | category | flops | bytes accessed | tf_op | source)
XLA Modules:
  0.0 148.7 jit_solution(29095569345746952)
XLA Ops:
  0.6 3.0 %collective-permute-start.5 = (f32[512,1280]{1,0:T(8,128)}, f32[512,1280]{1,0:T(8,128)S(1)}, u32[]{:S(2)}, u32[]{:S(2)}) collective-permute-start(f32[512,1280]{1,0:T(8,128)} %bitcast.5), channel_id=1, source_target_pairs={{16,0},{17,1},{18,2},{19,3},{20,4},{21,5},{22,6},{23,7},{9,8},{8,9... | collective-permute-start | bytes 7864328 | tf_op jit(solution)/shard_map/ppermute | solution.py:24
  3.7 1.5 %collective-permute-start.7 = (f32[512,1280]{1,0:T(8,128)}, f32[512,1280]{1,0:T(8,128)S(1)}, u32[]{:S(2)}, u32[]{:S(2)}) collective-permute-start(f32[512,1280]{1,0:T(8,128)} %bitcast.6), channel_id=1, source_target_pairs={{1,0},{0,1},{3,2},{2,3},{5,4},{4,5},{7,6},{6,7},{24,8},{25,9},{26,... | collective-permute-start | bytes 7864328 | tf_op jit(solution)/shard_map/ppermute | solution.py:24
  5.2 55.9 %collective-permute-done.5.first = f32[512,1280]{1,0:T(8,128)S(1)} collective-permute-done((f32[512,1280]{1,0:T(8,128)}, f32[512,1280]{1,0:T(8,128)S(1)}, u32[]{:S(2)}, u32[]{:S(2)}) %collective-permute-start.5) | collective-permute-done | bytes 2621472 | tf_op jit(solution)/shard_map/ppermute | solution.py:24
  61.7 2.4 %collective-permute-start.1 = (f32[1]{0:T(128)}, f32[1]{0:T(128)}, u32[]{:S(2)}, u32[]{:S(2)}) collective-permute-start(f32[1]{0:T(128)} %param.4), channel_id=1, source_target_pairs={{16,0},{17,1},{18,2},{19,3},{20,4},{21,5},{22,6},{23,7},{24,8},{25... | collective-permute-start | bytes 20 | tf_op jit(solution)/shard_map/ppermute | solution.py:24
  64.2 2.0 %collective-permute-done.e1 = f32[1]{0:T(128)} collective-permute-done((f32[1]{0:T(128)}, f32[1]{0:T(128)}, u32[]{:S(2)}, u32[]{:S(2)}) %collective-permute-start) | collective-permute-done | bytes 36 | tf_op jit(solution)/shard_map/ppermute | solution.py:24
  66.2 2.1 %collective-permute-start.2 = (f32[1]{0:T(128)}, f32[1]{0:T(128)}, u32[]{:S(2)}, u32[]{:S(2)}) collective-permute-start(f32[1]{0:T(128)} %param.4), channel_id=1, source_target_pairs={{24,0},{25,1},{26,2},{27,3},{28,4},{29,5},{30,6},{31,7},{16,8},{17... | collective-permute-start | bytes 20 | tf_op jit(solution)/shard_map/ppermute | solution.py:24
  69.8 1.1 collective-permute-start.11
  71.6 1.0 collective-permute-start.3
  72.6 12.2 %shard_map.50 = (f32[512,1280]{1,0:T(8,128)S(1)}, bf16[2,512,1280]{2,1,0:T(8,128)(2,1)S(1)}, bf16[2,512,1280]{2,1,0:T(8,128)(2,1)S(1)}, f32[8,512]{1,0:T(8,128)S(1)}, f32[512,1]{1,0:T(8,128)S(1)}) custom-call(f32[1]{0:T(128)S(6)} %copy.5.e0, f32[1]{0:T(128)} %collective-permute-done.e1, f32[1,512]{1,0:T(1,128)S(1)} %bitcast.9, f32[512,1280]{1,0:T(8,128)S(1)} %bitcast.8, ...), custom_call_target="tpu_custom_call" | custom-call | flops 8053063680 | bytes 8388608 | tf_op jit(solution)/shard_map/pallas_call | solution.py:248
  84.8 1.1 collective-permute-done.9.two_away
  85.9 14.0 %collective-permute-done.11.two_away = f32[256,1280]{1,0:T(8,128)S(1)} collective-permute-done((f32[256,1280]{1,0:T(8,128)S(1)}, f32[256,1280]{1,0:T(8,128)S(1)}, u32[]{:S(2)}, u32[]{:S(2)}) %collective-permute-start.11) | collective-permute-done | bytes 1310752 | tf_op jit(solution)/shard_map/ppermute | solution.py:24
  100.0 10.1 %shard_map.51 = (f32[512,1280]{1,0:T(8,128)S(1)}, bf16[2,512,1280]{2,1,0:T(8,128)(2,1)S(1)}, bf16[2,512,1280]{2,1,0:T(8,128)(2,1)S(1)}, f32[512,512]{1,0:T(8,128...) custom-call(f32[1]{0:T(128)S(6)} %copy.5.e0, f32[1]{0:T(128)} %collective-permute-done.e1, ...), custom_call_target="tpu_custom_call" | custom-call | flops 6039797760 | bytes 8388608 | tf_op jit(solution)/shard_map/pallas_call | solution.py:248
  110.1 2.7 %shard_map.52 = (bf16[2,512,1280]{2,1,0:T(8,128)(2,1)S(1)}, bf16[2,512,1280]{2,1,0:T(8,128)(2,1)S(1)}, f32[2,512,512]{2,1,0:T(8,128)S(1)}) custom-call(f32[8,512]{1,0:T(8,128)S(1)} %get-tuple-element.38.rows, f32[512,1]{1,0:T(8,128)S(1)} %get-tuple-element.36.col, bf16[2,512,1280]{2,1,0:T(8,128)(2,1)S(1)} %get-tuple-element.32.blocks_h, ...), custom_call_target="tpu_custom_call" | custom-call | flops 2013265920 | bytes 8388608 | tf_op jit(solution)/shard_map/pallas_call | solution.py:248
  112.9 10.2 %shard_map.53 = (bf16[2,512,1280]{2,1,0:T(8,128)(2,1)S(1)}, bf16[2,512,1280]{2,1,0:T(8,128)(2,1)S(1)}, bf16[3,512,512]{2,1,0:T(8,128)(2,1)S(1)}, bf16[3,512,512]...) custom-call(f32[8,512]{1,0:T(8,128)S(1)} %get-tuple-element.38.rows, ...), custom_call_target="tpu_custom_call" | custom-call | flops 8053063680 | bytes 8388608 | tf_op jit(solution)/shard_map/pallas_call | solution.py:248
  123.1 4.3 %shard_map.54.before = f32[512,1280]{1,0:T(8,128)S(1)} custom-call(f32[512,1280]{1,0:T(8,128)S(1)} %get-tuple-element.37.before, bf16[3,512,512]{2,1,0:T(8,128)(2,1)S(1)} %get-tuple-element.46.refs_0_.refs_4_, bf16[3,512,512]{2,1,0:T(8,128)(2,1)S(1)} %get-tuple-element.47.refs_1_.refs_5_, bf16[2,512,1280]{2,1,0:T(8,128)(2,1)S(1)} %get-tuple-element.42.pair_h.refs_2_, ...), custom_call_target="tpu_custom_call" | custom-call | flops 4026531840 | bytes 8388608 | tf_op jit(solution)/shard_map/pallas_call | solution.py:248
  127.4 2.2 %shard_map.55.before = f32[512,1280]{1,0:T(8,128)S(1)} custom-call(f32[512,1280]{1,0:T(8,128)S(1)} %shard_map.54.before, bf16[3,512,512]{2,1,0:T(8,128)(2,1)S(1)} %get-tuple-element.46.refs_0_.refs_4_, bf16[3,512,512]{2,1,0:T(8,128)(2,1)S(1)} %get-tuple-element.47.refs_1_.refs_5_, bf16[2,512,1280]{2,1,0:T(8,128)(2,1)S(1)} %get-tuple-element.48.refs_6_.refs_2_, ...), custom_call_target="tpu_custom_call" | custom-call | flops 2013265920 | bytes 8388608 | tf_op jit(solution)/shard_map/pallas_call | solution.py:248
  129.6 3.2 %shard_map.56 = (bf16[512,1280]{1,0:T(8,128)(2,1)S(1)}, bf16[512,1280]{1,0:T(8,128)(2,1)S(1)}, bf16[512,512]{1,0:T(8,128)(2,1)S(1)}, bf16[512,512]{1,0:T(8,128)(2,1)S(1)}, f32[8,512]{1,0:T(8,128)S(1)}) custom-call(f32[8,512]{1,0:T(8,128)S(1)} %get-tuple-element.38.rows, f32[512,1]{1,0:T(8,128)S(1)} %get-tuple-element.36.col, ...), custom_call_target="tpu_custom_call" | custom-call | flops 2013265920 | bytes 8388608 | tf_op jit(solution)/shard_map/pallas_call | solution.py:248
  132.8 3.0 %shard_map.58 = (bf16[512,1280]{1,0:T(8,128)(2,1)S(1)}, bf16[512,1280]{1,0:T(8,128)(2,1)S(1)}, bf16[512,512]{1,0:T(8,128)(2,1)S(1)}, bf16[512,512]{1,0:T(8,128)(2,1)S(1)}, f32[1,128]{1,0:T(1,128)S(1)}) custom-call(f32[8,512]{1,0:T(8,128)S(1)} %get-tuple-element.38.rows, f32[512,1]{1,0:T(8,128)S(1)} %get-tuple-element.36.col, ...), custom_call_target="tpu_custom_call" | custom-call | flops 2013265920 | bytes 8388608 | tf_op jit(solution)/shard_map/pallas_call | solution.py:248
  136.5 2.2 %shard_map.57.before = f32[512,1280]{1,0:T(8,128)S(1)} custom-call(f32[512,1280]{1,0:T(8,128)S(1)} %shard_map.55.before, bf16[512,512]{1,0:T(8,128)(2,1)S(1)} %get-tuple-element.52.refs_0_, bf16[512,512]{1,0:T(8,128)(2,1)S(1)} %get-tuple-element.53.refs_1_, bf16[512,1280]{1,0:T(8,128)(2,1)S(1)} %get-tuple-element.54.refs_2_, ...), custom_call_target="tpu_custom_call" | custom-call | flops 2013265920 | bytes 8388608 | tf_op jit(solution)/shard_map/pallas_call | solution.py:248
  139.4 1.6 %collective-permute-start.14 = (f32[1,128]{1,0:T(1,128)S(1)}, f32[1,128]{1,0:T(1,128)S(1)}, u32[]{:S(2)}, u32[]{:S(2)}) collective-permute-start(f32[1,128]{1,0:T(1,128)S(1)} %add.9), channel_id=1, source_target_pairs={{2,0},{3,1},{0,2},{1,3},{6,4},{7,5},{4,6},{5,7},{10,8},{11,9},{8,1... | collective-permute-start | bytes 1544 | tf_op jit(solution)/shard_map/ppermute | solution.py:24
  140.9 1.2 shard_map.59.before
  142.1 0.8 collective-permute-done.14
  142.9 2.6 %collective-permute-start.15 = (f32[1,128]{1,0:T(1,128)S(1)}, f32[1,128]{1,0:T(1,128)S(1)}, u32[]{:S(2)}, u32[]{:S(2)}) collective-permute-start(f32[1,128]{1,0:T(1,128)S(1)} %add.10), channel_id=1, source_target_pairs={{4,0},{5,1},{6,2},{7,3},{0,4},{1,5},{2,6},{3,7},{12,8},{13,9},{14,... | collective-permute-start | bytes 1544 | tf_op jit(solution)/shard_map/ppermute | solution.py:24
  145.5 2.7 %shard_map.60 = f32[512,1280]{1,0:T(8,128)} custom-call(f32[512,1280]{1,0:T(8,128)S(1)} %shard_map.59.before, bf16[512,512]{1,0:T(8,128)(2,1)S(1)} %get-tuple-element.57.refs_0_, bf16[512,512]{1,0:T(8,128)(2,1)S(1)} %get-tuple-element.58.refs_1_, bf16[512,1280]{1,0:T(8,128)(2,1)S(1)} %get-tuple-element.59.refs_2_, ...), custom_call_target="tpu_custom_call" | custom-call | flops 2013265920 | bytes 8388608 | tf_op jit(solution)/shard_map/pallas_call | solution.py:248
  (27 shorter events, 4.1 us)
Async XLA Ops:
  0.6 70.9 %copy-start.1 = (f32[512]{0:T(512)S(1)}, f32[512]{0:T(512)}, u32[]{:S(2)}) copy-start(f32[512]{0:T(512)} %param.5) | copy-start | bytes 6148
  0.6 71.9 %copy-start = (f32[1,512,1280]{2,1,0:T(8,128)S(1)}, f32[1,512,1280]{2,1,0:T(8,128)}, u32[]{:S(2)}) copy-start(f32[1,512,1280]{2,1,0:T(8,128)} %param.3) | copy-start | bytes 7864324
  0.6 60.5 %collective-permute-start.5 = (f32[512,1280]{1,0:T(8,128)}, f32[512,1280]{1,0:T(8,128)S(1)}, u32[]{:S(2)}, u32[]{:S(2)}) collective-permute-start(f32[512,1280]{1,0:T(8,128)} %bitcast.5), channel_id=1, source_target_pairs={{16,0},{17,1},{18,2},{19,3},{20,4},{21,5},{22,6},{23,7},{9,8},{8,9... | collective-permute-start | bytes 7864328 | tf_op jit(solution)/shard_map/ppermute | solution.py:24
  3.7 60.4 %collective-permute-start.7 = (f32[512,1280]{1,0:T(8,128)}, f32[512,1280]{1,0:T(8,128)S(1)}, u32[]{:S(2)}, u32[]{:S(2)}) collective-permute-start(f32[512,1280]{1,0:T(8,128)} %bitcast.6), channel_id=1, source_target_pairs={{1,0},{0,1},{3,2},{2,3},{5,4},{4,5},{7,6},{6,7},{24,8},{25,9},{26,... | collective-permute-start | bytes 7864328 | tf_op jit(solution)/shard_map/ppermute | solution.py:24
  5.2 66.3 %collective-permute-start.4 = (f32[512,1280]{1,0:T(8,128)}, f32[512,1280]{1,0:T(8,128)S(1)}, u32[]{:S(2)}, u32[]{:S(2)}) collective-permute-start(f32[512,1280]{1,0:T(8,128)} %bitcast.7), channel_id=1, source_target_pairs={{8,0},{9,1},{10,2},{11,3},{12,4},{13,5},{14,6},{15,7},{0,8},{1,9},... | collective-permute-start | bytes 7864328 | tf_op jit(solution)/shard_map/ppermute | solution.py:24
  61.1 38.9 %collective-permute-start.6 = (f32[512,1280]{1,0:T(8,128)S(1)}, f32[512,1280]{1,0:T(8,128)S(1)}, u32[]{:S(2)}, u32[]{:S(2)}) collective-permute-start(f32[512,1280]{1,0:T(8,128)S(1)} %collective-permute-done.5.first), channel_id=1, source_target_pairs={{8,0},{9,1},{10,2},{11,3},{12,4},{13,5},{14,6},{15,7},{0,8},{1,9},... | collective-permute-start | bytes 7864328 | tf_op jit(solution)/shard_map/ppermute | solution.py:24
  61.1 5.0 %collective-permute-start = (f32[1]{0:T(128)}, f32[1]{0:T(128)}, u32[]{:S(2)}, u32[]{:S(2)}) collective-permute-start(f32[1]{0:T(128)} %param.4), channel_id=1, source_target_pairs={{8,0},{9,1},{10,2},{11,3},{12,4},{13,5},{14,6},{15,7},{0,8},{1,9},... | collective-permute-start | bytes 20 | tf_op jit(solution)/shard_map/ppermute | solution.py:24
  61.7 6.7 %collective-permute-start.1 = (f32[1]{0:T(128)}, f32[1]{0:T(128)}, u32[]{:S(2)}, u32[]{:S(2)}) collective-permute-start(f32[1]{0:T(128)} %param.4), channel_id=1, source_target_pairs={{16,0},{17,1},{18,2},{19,3},{20,4},{21,5},{22,6},{23,7},{24,8},{25... | collective-permute-start | bytes 20 | tf_op jit(solution)/shard_map/ppermute | solution.py:24
  64.0 48.8 %collective-permute-start.8 = (f32[512,1280]{1,0:T(8,128)S(1)}, f32[512,1280]{1,0:T(8,128)S(1)}, u32[]{:S(2)}, u32[]{:S(2)}) collective-permute-start(f32[512,1280]{1,0:T(8,128)S(1)} %collective-permute-done.7.second), channel_id=1, source_target_pairs={{8,0},{9,1},{10,2},{11,3},{12,4},{13,5},{14,6},{15,7},{0,8},{1,9},... | collective-permute-start | bytes 7864328 | tf_op jit(solution)/shard_map/ppermute | solution.py:24
  66.2 3.6 %collective-permute-start.2 = (f32[1]{0:T(128)}, f32[1]{0:T(128)}, u32[]{:S(2)}, u32[]{:S(2)}) collective-permute-start(f32[1]{0:T(128)} %param.4), channel_id=1, source_target_pairs={{24,0},{25,1},{26,2},{27,3},{28,4},{29,5},{30,6},{31,7},{16,8},{17... | collective-permute-start | bytes 20 | tf_op jit(solution)/shard_map/ppermute | solution.py:24
  68.3 17.6 %collective-permute-start.9 = (f32[256,1280]{1,0:T(8,128)S(1)}, f32[256,1280]{1,0:T(8,128)S(1)}, u32[]{:S(2)}, u32[]{:S(2)}) collective-permute-start(f32[256,1280]{1,0:T(8,128)S(1)} %get-tuple-element.63), channel_id=1, source_target_pairs={{1,0},{0,1},{3,2},{2,3},{5,4},{4,5},{7,6},{6,7},{24,8},{25,9},{26,... | collective-permute-start | bytes 3932168 | tf_op jit(solution)/shard_map/ppermute | solution.py:24
  69.8 30.2 %collective-permute-start.11 = (f32[256,1280]{1,0:T(8,128)S(1)}, f32[256,1280]{1,0:T(8,128)S(1)}, u32[]{:S(2)}, u32[]{:S(2)}) collective-permute-start(f32[256,1280]{1,0:T(8,128)S(1)} %get-tuple-element.62), channel_id=1, source_target_pairs={{1,0},{0,1},{3,2},{2,3},{5,4},{4,5},{7,6},{6,7},{24,8},{25,9},{26,... | collective-permute-start | bytes 3932168 | tf_op jit(solution)/shard_map/ppermute | solution.py:24
  71.6 28.5 %collective-permute-start.3 = (f32[512]{0:T(512)S(1)}, f32[512]{0:T(512)S(1)}, u32[]{:S(2)}, u32[]{:S(2)}) collective-permute-start(f32[512]{0:T(512)S(1)} %copy-done.1), channel_id=1, source_target_pairs={{1,0},{0,1},{3,2},{2,3},{5,4},{4,5},{7,6},{6,7},{9,8},{8,9},{11,10... | collective-permute-start | bytes 6152 | tf_op jit(solution)/shard_map/ppermute | solution.py:24
  85.9 43.7 %collective-permute-start.10 = (f32[256,1280]{1,0:T(8,128)S(1)}, f32[256,1280]{1,0:T(8,128)S(1)}, u32[]{:S(2)}, u32[]{:S(2)}) collective-permute-start(f32[256,1280]{1,0:T(8,128)S(1)} %collective-permute-done.9.two_away), channel_id=1, source_target_pairs={{8,0},{9,1},{10,2},{11,3},{12,4},{13,5},{14,6},{15,7},{0,8},{1,9},... | collective-permute-start | bytes 3932168 | tf_op jit(solution)/shard_map/ppermute | solution.py:24
  100.0 32.8 %collective-permute-start.12 = (f32[256,1280]{1,0:T(8,128)S(1)}, f32[256,1280]{1,0:T(8,128)S(1)}, u32[]{:S(2)}, u32[]{:S(2)}) collective-permute-start(f32[256,1280]{1,0:T(8,128)S(1)} %collective-permute-done.11.two_away), channel_id=1, source_target_pairs={{8,0},{9,1},{10,2},{11,3},{12,4},{13,5},{14,6},{15,7},{0,8},{1,9},... | collective-permute-start | bytes 3932168 | tf_op jit(solution)/shard_map/ppermute | solution.py:24
  135.8 3.6 %collective-permute-start.13 = (f32[1,128]{1,0:T(1,128)S(1)}, f32[1,128]{1,0:T(1,128)S(1)}, u32[]{:S(2)}, u32[]{:S(2)}) collective-permute-start(f32[1,128]{1,0:T(1,128)S(1)} %get-tuple-element.61), channel_id=1, source_target_pairs={{1,0},{0,1},{3,2},{2,3},{5,4},{4,5},{7,6},{6,7},{9,8},{8,9},{11,10... | collective-permute-start | bytes 1544 | tf_op jit(solution)/shard_map/ppermute | solution.py:24
  139.4 3.6 %collective-permute-start.14 = (f32[1,128]{1,0:T(1,128)S(1)}, f32[1,128]{1,0:T(1,128)S(1)}, u32[]{:S(2)}, u32[]{:S(2)}) collective-permute-start(f32[1,128]{1,0:T(1,128)S(1)} %add.9), channel_id=1, source_target_pairs={{2,0},{3,1},{0,2},{1,3},{6,4},{7,5},{4,6},{5,7},{10,8},{11,9},{8,1... | collective-permute-start | bytes 1544 | tf_op jit(solution)/shard_map/ppermute | solution.py:24
  142.9 5.3 %collective-permute-start.15 = (f32[1,128]{1,0:T(1,128)S(1)}, f32[1,128]{1,0:T(1,128)S(1)}, u32[]{:S(2)}, u32[]{:S(2)}) collective-permute-start(f32[1,128]{1,0:T(1,128)S(1)} %add.10), channel_id=1, source_target_pairs={{4,0},{5,1},{6,2},{7,3},{0,4},{1,5},{2,6},{3,7},{12,8},{13,9},{14,... | collective-permute-start | bytes 1544 | tf_op jit(solution)/shard_map/ppermute | solution.py:24

commit v4 on v3

--- a/solution.py
+++ b/solution.py
@@ -77,6 +77,12 @@
         high[m], low[m] = split(rows[m])
 
     each(rows.shape[0], step, 4)
+
+
+def by_offset(sums, factor):
+    lane = lax.broadcasted_iota(jnp.int32, (1, 128), 1)
+    terms = [sums[0], jnp.where(is_odd() == 1, sums[1], sums[3]), sums[2]]
+    return sum(jnp.where(lane == k, term * factor, 0.0) for k, term in enumerate(terms))
 
 
 def start_kernel(weights, e0, e1, vir, own, near, total, blocks_h, blocks_l, traces, col,
@@ -156,9 +162,9 @@
     each(n, step, 1)
 
 
-def amps_kernel(weights, rows, col, blocks_h, blocks_l, pair_h, pair_l, amps,
+def amps_kernel(weights, factor, rows, col, blocks_h, blocks_l, pair_h, pair_l, amps,
                 firsts_h, firsts_l, second_core, traces_in,
-                rest_h, rest_l, bars_h, bars_l, crosses, traces, rest_amp):
+                rest_h, rest_l, bars_h, bars_l, crosses, trace, rest_amp, traces):
     n = second_core.shape[0]
     odd = is_odd()
     put_split(rest_h.at[1 - odd], rest_l.at[1 - odd], second_core)
@@ -189,6 +195,8 @@
     traces[pl.ds(3 - odd, 1)] = lanes(amp * bar)
     scale = jnp.where(odd == 0, float(weights[1]), float(weights[2]))
     bars_h[2], bars_l[2] = split(scale * bar)
+    trace[...] = by_offset(
+        [jnp.sum(traces[k : k + 1], axis=1, keepdims=True) for k in range(4)], factor)
 
 
 def add_kernel(terms, before, *refs):
@@ -207,7 +215,10 @@
 
 
 def part_kernel(weights, start, factor, rows, col, blocks_h, blocks_l, two_away, three_away,
-                crosses, traces_in, rows_h, rows_l, bar_h, bar_l, traces, sums):
+                crosses, *refs):
+    before, trace_in, trace_far = refs[:3] if factor else (None, None, None)
+    rows_h, rows_l, bar_h, bar_l, out = refs[-6:-1] if factor else refs[-5:]
+    sums = refs[-1]
     size = two_away.shape[0]
     put_split(rows_h.at[:size], rows_l.at[:size], two_away)
     put_split(rows_h.at[size:], rows_l.at[size:], three_away)
@@ -215,28 +226,22 @@
     row = jnp.concatenate([rows[2:3, part], rows[3:4, part]], axis=1)
     lane = lax.broadcasted_iota(jnp.int32, (1, 2 * size), 1)
     scale = jnp.where(lane < size, float(weights[2]), float(weights[1]))
-    sums[...] = jnp.zeros(sums.shape, F32)
+    sums[...] = before[...] if factor else jnp.zeros(sums.shape, F32)
 
     def step(m):
         amp = product((blocks_h[0, m], blocks_l[0, m]), (rows_h[...], rows_l[...]), True) / (row - col[m])
-        bar = 2.0 * amp - jnp.concatenate([crosses[0, m, part], crosses[1, m, part]], axis=1)
-        sums[...] += lanes(amp * bar)
+        cross = jnp.concatenate([crosses[0, m, part], crosses[1, m, part]], axis=1)
+        bar = 2.0 * amp - cross
+        sums[...] += lanes(amp * bar + cross * (2.0 * cross - amp))
         bar_h[m], bar_l[m] = split(scale * bar)
 
     each(col.shape[0], step, 1)
-    two, three = sums[:, :size], sums[:, size:]
-    if factor is None:
-        traces[...] = traces_in[...]
-        traces[2:3, :size] += two
-        traces[3:4, :size] += three
+    if not factor:
         return
-    odd = is_odd()
-    whole = [jnp.sum(traces_in[k : k + 1], axis=1, keepdims=True) for k in range(4)]
-    whole[2] += jnp.sum(two, axis=1, keepdims=True)
-    whole[3] += jnp.sum(three, axis=1, keepdims=True)
-    lane = lax.broadcasted_iota(jnp.int32, (1, 128), 1)
-    by_offset = [whole[0], jnp.where(odd == 1, whole[1], whole[3]), whole[2]]
-    traces[...] = sum(jnp.where(lane == k, by_offset[k], 0.0) for k in range(3)) * factor
+    two = jnp.sum(sums[:, :size], axis=1, keepdims=True)
+    three = jnp.sum(sums[:, size:], axis=1, keepdims=True)
+    zero = jnp.zeros_like(two)
+    out[...] = trace_in[...] + trace_far[...] + by_offset([zero, zero, two, three], factor)
 
 
 VMEM = pl.BlockSpec(memory_space=pltpu.VMEM)
@@ -305,11 +310,13 @@
     *pair, amps = call(
         middle_kernel, 1,
         [gap_rows, col, *blocks, *firsts, far_amp, second], [*doubles, ((2, *square), F32)], [])
-    *rest, bars_h, bars_l, crosses, traces = call(
-        functools.partial(amps_kernel, weights), 4,
+    scale = 1.0 / (rows * lax.axis_size("vir"))
+    *rest, bars_h, bars_l, crosses, trace = call(
+        functools.partial(amps_kernel, weights, scale), 4,
         [gap_rows, col, *blocks, *pair, amps, *firsts, second_core, traces],
-        [*doubles, ((3, *square), BF16), ((3, *square), BF16), ((2, *square), F32), lines],
-        [pltpu.VMEM((2, *square), F32)])
+        [*doubles, ((3, *square), BF16), ((3, *square), BF16), ((2, *square), F32), ((1, 128), F32)],
+        [pltpu.VMEM((2, *square), F32), pltpu.VMEM((8, rows), F32)])
+    trace_far = permuted(trace, lambda i, v: (i, v ^ 1))
 
     def add(before, *terms, span=slice(None)):
         slots = tuple((bar_slot, block_slot, span) for bar_slot, _, block_slot, _ in terms)
@@ -317,24 +324,24 @@
         return call(
             functools.partial(add_kernel, slots), len(terms), [before, *arrays], [dense], [])[0]
 
-    def part(start, factor, two_away, three_away, traces):
-        out = lines if factor is None else ((1, 128), F32)
-        *parts, bar_h, bar_l, traces = call(
+    def part(start, factor, two_away, three_away, *more):
+        out, scratch = (((1, 128), F32), [sums]) if factor else (((1, 2 * half), F32), [])
+        *parts, bar_h, bar_l, out = call(
             functools.partial(part_kernel, weights, start, factor), 1,
-            [gap_rows, col, *blocks, two_away, three_away, crosses, traces],
-            [((2 * half, aux), BF16)] * 2 + [((rows, 2 * half), BF16)] * 2 + [out], [sums])
-        return parts, (bar_h, bar_l), traces
+            [gap_rows, col, *blocks, two_away, three_away, crosses, *more],
+            [((2 * half, aux), BF16)] * 2 + [((rows, 2 * half), BF16)] * 2 + [out], scratch)
+        return parts, (bar_h, bar_l), out
 
     all_bars = (bars_h, bars_l)
     density = add(density, (0, all_bars, 0, pair), (1, all_bars, 0, rest))
-    part_0, part_bars_0, traces = part(0, None, low_part, low_core, traces)
+    part_0, part_bars_0, part_sums = part(0, None, low_part, low_core)
     density = add(density, (2, all_bars, 1, rest))
     density = add(density, (None, part_bars_0, None, part_0))
-    scale = 1.0 / (rows * lax.axis_size("vir"))
-    part_1, part_bars_1, traces = part(half, scale, high_part, high_core, traces)
+    part_1, part_bars_1, trace = part(
+        half, scale, high_part, high_core, part_sums, trace, trace_far)
     density = add(density, (None, part_bars_1, None, part_1), span=slice(0, half))
     density = add(density, (None, part_bars_1, None, part_1), span=slice(half, 2 * half))
-    return density[None], traces
+    return density[None], trace
 
 
 def contract(pattern, former, latter):
@@ -376,7 +383,7 @@
     nvir = factor.shape[1] * virs
     if gathered is gathered_ring:
         return density, lax.psum(traces[None] / nvir, "vir")
-    apart = 1
+    apart = 2
     while apart < virs:
         traces = traces + permuted(traces, lambda i, v: (i, v ^ apart))
         apart *= 2

time: 149 us -> 149 us (level)
  transfers between devices with their start and end apart: 16 -> 16, of which waited for: 7 -> 6; matrix products, arithmetic and copies ran while one was open for 0% -> 0% of each run, Pallas kernels for 34% -> 35%
where the time goes in v4:
time: 149 us
  waiting for transfers between devices  74.7 us (50%)
  Pallas kernels  54.4 us (37%)
  starting transfers between devices  17.3 us (12%)
    ppermute x16, waiting for transfers between devices, permuted(): return lax.ppermute(value, AXES, route)  74.7 us
    pallas_call x11, Pallas kernels, call(): pl.pallas_call(kernel, in_specs=[SMEM if value.size == 1 else VMEM for va...  54.4 us
    ppermute x16, starting transfers between devices, permuted(): return lax.ppermute(value, AXES, route)  17.3 us
  transfers between devices with their start and end apart: 16, of which 6 were waited for; matrix products, arithmetic and copies ran while one was open for 0% of the time, Pallas kernels for 35%

profile of v4, /device:TPU:0, one launch (start us, length us, event | category | flops | bytes accessed | tf_op | source)
XLA Modules:
  0.0 148.5 jit_solution(11395804689340129736)
XLA Ops:
  0.6 3.0 %collective-permute-start.5 = (f32[512,1280]{1,0:T(8,128)}, f32[512,1280]{1,0:T(8,128)S(1)}, u32[]{:S(2)}, u32[]{:S(2)}) collective-permute-start(f32[512,1280]{1,0:T(8,128)} %bitcast.5), channel_id=1, source_target_pairs={{16,0},{17,1},{18,2},{19,3},{20,4},{21,5},{22,6},{23,7},{9,8},{8,9... | collective-permute-start | bytes 7864328 | tf_op jit(solution)/shard_map/ppermute | solution.py:24
  3.7 1.5 %collective-permute-start.7 = (f32[512,1280]{1,0:T(8,128)}, f32[512,1280]{1,0:T(8,128)S(1)}, u32[]{:S(2)}, u32[]{:S(2)}) collective-permute-start(f32[512,1280]{1,0:T(8,128)} %bitcast.6), channel_id=1, source_target_pairs={{1,0},{0,1},{3,2},{2,3},{5,4},{4,5},{7,6},{6,7},{24,8},{25,9},{26,... | collective-permute-start | bytes 7864328 | tf_op jit(solution)/shard_map/ppermute | solution.py:24
  5.2 55.9 %collective-permute-done.5.first = f32[512,1280]{1,0:T(8,128)S(1)} collective-permute-done((f32[512,1280]{1,0:T(8,128)}, f32[512,1280]{1,0:T(8,128)S(1)}, u32[]{:S(2)}, u32[]{:S(2)}) %collective-permute-start.5) | collective-permute-done | bytes 2621472 | tf_op jit(solution)/shard_map/ppermute | solution.py:24
  61.7 2.4 %collective-permute-start.1 = (f32[1]{0:T(128)}, f32[1]{0:T(128)}, u32[]{:S(2)}, u32[]{:S(2)}) collective-permute-start(f32[1]{0:T(128)} %param.4), channel_id=1, source_target_pairs={{16,0},{17,1},{18,2},{19,3},{20,4},{21,5},{22,6},{23,7},{24,8},{25... | collective-permute-start | bytes 20 | tf_op jit(solution)/shard_map/ppermute | solution.py:24
  64.2 2.0 %collective-permute-done.e1 = f32[1]{0:T(128)} collective-permute-done((f32[1]{0:T(128)}, f32[1]{0:T(128)}, u32[]{:S(2)}, u32[]{:S(2)}) %collective-permute-start) | collective-permute-done | bytes 36 | tf_op jit(solution)/shard_map/ppermute | solution.py:24
  66.2 2.1 %collective-permute-start.2 = (f32[1]{0:T(128)}, f32[1]{0:T(128)}, u32[]{:S(2)}, u32[]{:S(2)}) collective-permute-start(f32[1]{0:T(128)} %param.4), channel_id=1, source_target_pairs={{24,0},{25,1},{26,2},{27,3},{28,4},{29,5},{30,6},{31,7},{16,8},{17... | collective-permute-start | bytes 20 | tf_op jit(solution)/shard_map/ppermute | solution.py:24
  69.8 1.1 collective-permute-start.11
  71.6 1.0 collective-permute-start.3
  72.6 12.3 %shard_map.50 = (f32[512,1280]{1,0:T(8,128)S(1)}, bf16[2,512,1280]{2,1,0:T(8,128)(2,1)S(1)}, bf16[2,512,1280]{2,1,0:T(8,128)(2,1)S(1)}, f32[8,512]{1,0:T(8,128)S(1)}, f32[512,1]{1,0:T(8,128)S(1)}) custom-call(f32[1]{0:T(128)S(6)} %copy.5.e0, f32[1]{0:T(128)} %collective-permute-done.e1, f32[1,512]{1,0:T(1,128)S(1)} %bitcast.9, f32[512,1280]{1,0:T(8,128)S(1)} %bitcast.8, ...), custom_call_target="tpu_custom_call" | custom-call | flops 8053063680 | bytes 8388608 | tf_op jit(solution)/shard_map/pallas_call | solution.py:253
  84.8 1.1 collective-permute-done.9.two_away
  85.9 14.0 %collective-permute-done.11.two_away = f32[256,1280]{1,0:T(8,128)S(1)} collective-permute-done((f32[256,1280]{1,0:T(8,128)S(1)}, f32[256,1280]{1,0:T(8,128)S(1)}, u32[]{:S(2)}, u32[]{:S(2)}) %collective-permute-start.11) | collective-permute-done | bytes 1310752 | tf_op jit(solution)/shard_map/ppermute | solution.py:24
  100.0 10.1 %shard_map.51 = (f32[512,1280]{1,0:T(8,128)S(1)}, bf16[2,512,1280]{2,1,0:T(8,128)(2,1)S(1)}, bf16[2,512,1280]{2,1,0:T(8,128)(2,1)S(1)}, f32[512,512]{1,0:T(8,128...) custom-call(f32[1]{0:T(128)S(6)} %copy.5.e0, f32[1]{0:T(128)} %collective-permute-done.e1, ...), custom_call_target="tpu_custom_call" | custom-call | flops 6039797760 | bytes 8388608 | tf_op jit(solution)/shard_map/pallas_call | solution.py:253
  110.2 2.7 %shard_map.52 = (bf16[2,512,1280]{2,1,0:T(8,128)(2,1)S(1)}, bf16[2,512,1280]{2,1,0:T(8,128)(2,1)S(1)}, f32[2,512,512]{2,1,0:T(8,128)S(1)}) custom-call(f32[8,512]{1,0:T(8,128)S(1)} %get-tuple-element.38.rows, f32[512,1]{1,0:T(8,128)S(1)} %get-tuple-element.36.col, bf16[2,512,1280]{2,1,0:T(8,128)(2,1)S(1)} %get-tuple-element.32.blocks_h, ...), custom_call_target="tpu_custom_call" | custom-call | flops 2013265920 | bytes 8388608 | tf_op jit(solution)/shard_map/pallas_call | solution.py:253
  112.9 10.2 %shard_map.53 = (bf16[2,512,1280]{2,1,0:T(8,128)(2,1)S(1)}, bf16[2,512,1280]{2,1,0:T(8,128)(2,1)S(1)}, bf16[3,512,512]{2,1,0:T(8,128)(2,1)S(1)}, bf16[3,512,512]...) custom-call(f32[8,512]{1,0:T(8,128)S(1)} %get-tuple-element.38.rows, ...), custom_call_target="tpu_custom_call" | custom-call | flops 8053063680 | bytes 8388608 | tf_op jit(solution)/shard_map/pallas_call | solution.py:253
  123.1 0.8 collective-permute-start.13
  123.9 4.3 %shard_map.54.before = f32[512,1280]{1,0:T(8,128)S(1)} custom-call(f32[512,1280]{1,0:T(8,128)S(1)} %get-tuple-element.37.before, bf16[3,512,512]{2,1,0:T(8,128)(2,1)S(1)} %get-tuple-element.46.refs_0_.refs_4_, bf16[3,512,512]{2,1,0:T(8,128)(2,1)S(1)} %get-tuple-element.47.refs_1_.refs_5_, bf16[2,512,1280]{2,1,0:T(8,128)(2,1)S(1)} %get-tuple-element.42.pair_h.refs_2_, ...), custom_call_target="tpu_custom_call" | custom-call | flops 4026531840 | bytes 8388608 | tf_op jit(solution)/shard_map/pallas_call | solution.py:253
  128.3 2.2 %shard_map.55.before = f32[512,1280]{1,0:T(8,128)S(1)} custom-call(f32[512,1280]{1,0:T(8,128)S(1)} %shard_map.54.before, bf16[3,512,512]{2,1,0:T(8,128)(2,1)S(1)} %get-tuple-element.46.refs_0_.refs_4_, bf16[3,512,512]{2,1,0:T(8,128)(2,1)S(1)} %get-tuple-element.47.refs_1_.refs_5_, bf16[2,512,1280]{2,1,0:T(8,128)(2,1)S(1)} %get-tuple-element.48.refs_6_.refs_2_, ...), custom_call_target="tpu_custom_call" | custom-call | flops 2013265920 | bytes 8388608 | tf_op jit(solution)/shard_map/pallas_call | solution.py:253
  130.5 3.3 %shard_map.56 = (bf16[512,1280]{1,0:T(8,128)(2,1)S(1)}, bf16[512,1280]{1,0:T(8,128)(2,1)S(1)}, bf16[512,512]{1,0:T(8,128)(2,1)S(1)}, bf16[512,512]{1,0:T(8,128)(2,1)S(1)}, f32[1,512]{1,0:T(1,128)S(1)}) custom-call(f32[8,512]{1,0:T(8,128)S(1)} %get-tuple-element.38.rows, f32[512,1]{1,0:T(8,128)S(1)} %get-tuple-element.36.col, ...), custom_call_target="tpu_custom_call" | custom-call | flops 2013265920 | bytes 8388608 | tf_op jit(solution)/shard_map/pallas_call | solution.py:253
  133.8 2.2 %shard_map.57.before = f32[512,1280]{1,0:T(8,128)S(1)} custom-call(f32[512,1280]{1,0:T(8,128)S(1)} %shard_map.55.before, bf16[512,512]{1,0:T(8,128)(2,1)S(1)} %get-tuple-element.51.refs_0_, bf16[512,512]{1,0:T(8,128)(2,1)S(1)} %get-tuple-element.52.refs_1_, bf16[512,1280]{1,0:T(8,128)(2,1)S(1)} %get-tuple-element.53.refs_2_, ...), custom_call_target="tpu_custom_call" | custom-call | flops 2013265920 | bytes 8388608 | tf_op jit(solution)/shard_map/pallas_call | solution.py:253
  136.0 3.1 %shard_map.58 = (bf16[512,1280]{1,0:T(8,128)(2,1)S(1)}, bf16[512,1280]{1,0:T(8,128)(2,1)S(1)}, bf16[512,512]{1,0:T(8,128)(2,1)S(1)}, bf16[512,512]{1,0:T(8,128)(2,1)S(1)}, f32[1,128]{1,0:T(1,128)S(1)}) custom-call(f32[8,512]{1,0:T(8,128)S(1)} %get-tuple-element.38.rows, f32[512,1]{1,0:T(8,128)S(1)} %get-tuple-element.36.col, ...), custom_call_target="tpu_custom_call" | custom-call | flops 2013265920 | bytes 8388608 | tf_op jit(solution)/shard_map/pallas_call | solution.py:253
  139.2 1.6 %collective-permute-start.14 = (f32[1,128]{1,0:T(1,128)S(1)}, f32[1,128]{1,0:T(1,128)S(1)}, u32[]{:S(2)}, u32[]{:S(2)}) collective-permute-start(f32[1,128]{1,0:T(1,128)S(1)} %get-tuple-element.61), channel_id=1, source_target_pairs={{2,0},{3,1},{0,2},{1,3},{6,4},{7,5},{4,6},{5,7},{10,8},{11,9},{8,1... | collective-permute-start | bytes 1544 | tf_op jit(solution)/shard_map/ppermute | solution.py:24
  140.8 1.2 shard_map.59.before
  142.8 2.6 %collective-permute-start.15 = (f32[1,128]{1,0:T(1,128)S(1)}, f32[1,128]{1,0:T(1,128)S(1)}, u32[]{:S(2)}, u32[]{:S(2)}) collective-permute-start(f32[1,128]{1,0:T(1,128)S(1)} %add.6), channel_id=1, source_target_pairs={{4,0},{5,1},{6,2},{7,3},{0,4},{1,5},{2,6},{3,7},{12,8},{13,9},{14,... | collective-permute-start | bytes 1544 | tf_op jit(solution)/shard_map/ppermute | solution.py:24
  145.3 2.7 %shard_map.60 = f32[512,1280]{1,0:T(8,128)} custom-call(f32[512,1280]{1,0:T(8,128)S(1)} %shard_map.59.before, bf16[512,512]{1,0:T(8,128)(2,1)S(1)} %get-tuple-element.57.refs_0_, bf16[512,512]{1,0:T(8,128)(2,1)S(1)} %get-tuple-element.58.refs_1_, bf16[512,1280]{1,0:T(8,128)(2,1)S(1)} %get-tuple-element.59.refs_2_, ...), custom_call_target="tpu_custom_call" | custom-call | flops 2013265920 | bytes 8388608 | tf_op jit(solution)/shard_map/pallas_call | solution.py:253
  (26 shorter events, 3.5 us)
Async XLA Ops:
  0.6 70.9 %copy-start.1 = (f32[512]{0:T(512)S(1)}, f32[512]{0:T(512)}, u32[]{:S(2)}) copy-start(f32[512]{0:T(512)} %param.5) | copy-start | bytes 6148
  0.6 71.9 %copy-start = (f32[1,512,1280]{2,1,0:T(8,128)S(1)}, f32[1,512,1280]{2,1,0:T(8,128)}, u32[]{:S(2)}) copy-start(f32[1,512,1280]{2,1,0:T(8,128)} %param.3) | copy-start | bytes 7864324
  0.6 60.5 %collective-permute-start.5 = (f32[512,1280]{1,0:T(8,128)}, f32[512,1280]{1,0:T(8,128)S(1)}, u32[]{:S(2)}, u32[]{:S(2)}) collective-permute-start(f32[512,1280]{1,0:T(8,128)} %bitcast.5), channel_id=1, source_target_pairs={{16,0},{17,1},{18,2},{19,3},{20,4},{21,5},{22,6},{23,7},{9,8},{8,9... | collective-permute-start | bytes 7864328 | tf_op jit(solution)/shard_map/ppermute | solution.py:24
  3.7 60.4 %collective-permute-start.7 = (f32[512,1280]{1,0:T(8,128)}, f32[512,1280]{1,0:T(8,128)S(1)}, u32[]{:S(2)}, u32[]{:S(2)}) collective-permute-start(f32[512,1280]{1,0:T(8,128)} %bitcast.6), channel_id=1, source_target_pairs={{1,0},{0,1},{3,2},{2,3},{5,4},{4,5},{7,6},{6,7},{24,8},{25,9},{26,... | collective-permute-start | bytes 7864328 | tf_op jit(solution)/shard_map/ppermute | solution.py:24
  5.2 66.3 %collective-permute-start.4 = (f32[512,1280]{1,0:T(8,128)}, f32[512,1280]{1,0:T(8,128)S(1)}, u32[]{:S(2)}, u32[]{:S(2)}) collective-permute-start(f32[512,1280]{1,0:T(8,128)} %bitcast.7), channel_id=1, source_target_pairs={{8,0},{9,1},{10,2},{11,3},{12,4},{13,5},{14,6},{15,7},{0,8},{1,9},... | collective-permute-start | bytes 7864328 | tf_op jit(solution)/shard_map/ppermute | solution.py:24
  61.1 38.9 %collective-permute-start.6 = (f32[512,1280]{1,0:T(8,128)S(1)}, f32[512,1280]{1,0:T(8,128)S(1)}, u32[]{:S(2)}, u32[]{:S(2)}) collective-permute-start(f32[512,1280]{1,0:T(8,128)S(1)} %collective-permute-done.5.first), channel_id=1, source_target_pairs={{8,0},{9,1},{10,2},{11,3},{12,4},{13,5},{14,6},{15,7},{0,8},{1,9},... | collective-permute-start | bytes 7864328 | tf_op jit(solution)/shard_map/ppermute | solution.py:24
  61.1 5.0 %collective-permute-start = (f32[1]{0:T(128)}, f32[1]{0:T(128)}, u32[]{:S(2)}, u32[]{:S(2)}) collective-permute-start(f32[1]{0:T(128)} %param.4), channel_id=1, source_target_pairs={{8,0},{9,1},{10,2},{11,3},{12,4},{13,5},{14,6},{15,7},{0,8},{1,9},... | collective-permute-start | bytes 20 | tf_op jit(solution)/shard_map/ppermute | solution.py:24
  61.7 6.7 %collective-permute-start.1 = (f32[1]{0:T(128)}, f32[1]{0:T(128)}, u32[]{:S(2)}, u32[]{:S(2)}) collective-permute-start(f32[1]{0:T(128)} %param.4), channel_id=1, source_target_pairs={{16,0},{17,1},{18,2},{19,3},{20,4},{21,5},{22,6},{23,7},{24,8},{25... | collective-permute-start | bytes 20 | tf_op jit(solution)/shard_map/ppermute | solution.py:24
  64.0 48.9 %collective-permute-start.8 = (f32[512,1280]{1,0:T(8,128)S(1)}, f32[512,1280]{1,0:T(8,128)S(1)}, u32[]{:S(2)}, u32[]{:S(2)}) collective-permute-start(f32[512,1280]{1,0:T(8,128)S(1)} %collective-permute-done.7.second), channel_id=1, source_target_pairs={{8,0},{9,1},{10,2},{11,3},{12,4},{13,5},{14,6},{15,7},{0,8},{1,9},... | collective-permute-start | bytes 7864328 | tf_op jit(solution)/shard_map/ppermute | solution.py:24
  66.2 3.6 %collective-permute-start.2 = (f32[1]{0:T(128)}, f32[1]{0:T(128)}, u32[]{:S(2)}, u32[]{:S(2)}) collective-permute-start(f32[1]{0:T(128)} %param.4), channel_id=1, source_target_pairs={{24,0},{25,1},{26,2},{27,3},{28,4},{29,5},{30,6},{31,7},{16,8},{17... | collective-permute-start | bytes 20 | tf_op jit(solution)/shard_map/ppermute | solution.py:24
  68.3 17.6 %collective-permute-start.9 = (f32[256,1280]{1,0:T(8,128)S(1)}, f32[256,1280]{1,0:T(8,128)S(1)}, u32[]{:S(2)}, u32[]{:S(2)}) collective-permute-start(f32[256,1280]{1,0:T(8,128)S(1)} %get-tuple-element.63), channel_id=1, source_target_pairs={{1,0},{0,1},{3,2},{2,3},{5,4},{4,5},{7,6},{6,7},{24,8},{25,9},{26,... | collective-permute-start | bytes 3932168 | tf_op jit(solution)/shard_map/ppermute | solution.py:24
  69.8 30.2 %collective-permute-start.11 = (f32[256,1280]{1,0:T(8,128)S(1)}, f32[256,1280]{1,0:T(8,128)S(1)}, u32[]{:S(2)}, u32[]{:S(2)}) collective-permute-start(f32[256,1280]{1,0:T(8,128)S(1)} %get-tuple-element.62), channel_id=1, source_target_pairs={{1,0},{0,1},{3,2},{2,3},{5,4},{4,5},{7,6},{6,7},{24,8},{25,9},{26,... | collective-permute-start | bytes 3932168 | tf_op jit(solution)/shard_map/ppermute | solution.py:24
  71.6 28.5 %collective-permute-start.3 = (f32[512]{0:T(512)S(1)}, f32[512]{0:T(512)S(1)}, u32[]{:S(2)}, u32[]{:S(2)}) collective-permute-start(f32[512]{0:T(512)S(1)} %copy-done.1), channel_id=1, source_target_pairs={{1,0},{0,1},{3,2},{2,3},{5,4},{4,5},{7,6},{6,7},{9,8},{8,9},{11,10... | collective-permute-start | bytes 6152 | tf_op jit(solution)/shard_map/ppermute | solution.py:24
  85.9 44.6 %collective-permute-start.10 = (f32[256,1280]{1,0:T(8,128)S(1)}, f32[256,1280]{1,0:T(8,128)S(1)}, u32[]{:S(2)}, u32[]{:S(2)}) collective-permute-start(f32[256,1280]{1,0:T(8,128)S(1)} %collective-permute-done.9.two_away), channel_id=1, source_target_pairs={{8,0},{9,1},{10,2},{11,3},{12,4},{13,5},{14,6},{15,7},{0,8},{1,9},... | collective-permute-start | bytes 3932168 | tf_op jit(solution)/shard_map/ppermute | solution.py:24
  100.0 36.0 %collective-permute-start.12 = (f32[256,1280]{1,0:T(8,128)S(1)}, f32[256,1280]{1,0:T(8,128)S(1)}, u32[]{:S(2)}, u32[]{:S(2)}) collective-permute-start(f32[256,1280]{1,0:T(8,128)S(1)} %collective-permute-done.11.two_away), channel_id=1, source_target_pairs={{8,0},{9,1},{10,2},{11,3},{12,4},{13,5},{14,6},{15,7},{0,8},{1,9},... | collective-permute-start | bytes 3932168 | tf_op jit(solution)/shard_map/ppermute | solution.py:24
  123.1 12.9 %collective-permute-start.13 = (f32[1,128]{1,0:T(1,128)S(1)}, f32[1,128]{1,0:T(1,128)S(1)}, u32[]{:S(2)}, u32[]{:S(2)}) collective-permute-start(f32[1,128]{1,0:T(1,128)S(1)} %get-tuple-element.56.refs_1_), channel_id=1, source_target_pairs={{1,0},{0,1},{3,2},{2,3},{5,4},{4,5},{7,6},{6,7},{9,8},{8,9},{11,10... | collective-permute-start | bytes 1544 | tf_op jit(solution)/shard_map/ppermute | solution.py:24
  139.2 3.6 %collective-permute-start.14 = (f32[1,128]{1,0:T(1,128)S(1)}, f32[1,128]{1,0:T(1,128)S(1)}, u32[]{:S(2)}, u32[]{:S(2)}) collective-permute-start(f32[1,128]{1,0:T(1,128)S(1)} %get-tuple-element.61), channel_id=1, source_target_pairs={{2,0},{3,1},{0,2},{1,3},{6,4},{7,5},{4,6},{5,7},{10,8},{11,9},{8,1... | collective-permute-start | bytes 1544 | tf_op jit(solution)/shard_map/ppermute | solution.py:24
  142.8 5.3 %collective-permute-start.15 = (f32[1,128]{1,0:T(1,128)S(1)}, f32[1,128]{1,0:T(1,128)S(1)}, u32[]{:S(2)}, u32[]{:S(2)}) collective-permute-start(f32[1,128]{1,0:T(1,128)S(1)} %add.6), channel_id=1, source_target_pairs={{4,0},{5,1},{6,2},{7,3},{0,4},{1,5},{2,6},{3,7},{12,8},{13,9},{14,... | collective-permute-start | bytes 1544 | tf_op jit(solution)/shard_map/ppermute | solution.py:24
